TPU v7x, 32 devices: a whole 2x2x4 slice. The times are simulated.
32 devices in a mesh: dp: 2 (over x), tp: 4 (over z), cp: 4 (over y, core).
Axes of the slice: x: 2, y: 2, z: 4, core: 2. Of those that a mesh axis runs over, the one named last changes fastest.
Arguments:
- x_in: bfloat16 [16384, 4096], P(('dp', 'cp', 'tp')), parts along dimension 0
- seg_ids: int32 [16384], P(('dp', 'cp', 'tp')), parts along dimension 0
- w_q: bfloat16 [4096, 32, 128], P(None, 'tp')
- w_k: bfloat16 [4096, 8, 128], P(None, 'tp')
- w_v: bfloat16 [4096, 8, 128], P(None, 'tp')
- w_o: bfloat16 [32, 128, 4096], P('tp')
Outputs:
- output: bfloat16 [16384, 4096], P(('dp', 'cp', 'tp')), parts along dimension 0
There are 2 independent parts. A program takes and returns all parts, laid end to end along the dimension named above; an argument that names none is the same for every part.
All inputs are finite; a program needn't handle non-finite values.
Results may differ from a plain program's by a relative error of at most 0.00421059.
Values are sent between devices in bfloat16 or wider.
A program may use at most 1 GiB of HBM per device.

v0:
```python
import jax
import jax.numpy as jnp
from jax import lax
from jax.sharding import PartitionSpec as P

NEG_BIG = -1e30


def block_update(softmax_state, q_blk, k_blk, v_blk, allowed, logit_scale):
    m_old, l_old, acc_old = softmax_state
    scores = jnp.einsum("qkge,ske->kgqs", q_blk, k_blk, preferred_element_type=jnp.float32) * logit_scale
    scores = jnp.where(allowed, scores, NEG_BIG)
    m_new = jnp.maximum(m_old, jnp.max(scores, axis=-1))
    prob_blk = jnp.exp(scores - m_new[..., None])
    rescale = jnp.exp(m_old - m_new)
    pv_part = jnp.einsum("kgqs,ske->kgqe", prob_blk.astype(jnp.bfloat16), v_blk, preferred_element_type=jnp.float32)
    return m_new, rescale * l_old + jnp.sum(prob_blk, axis=-1), rescale[..., None] * acc_old + pv_part


def visible_mask(pos_q, seg_q, pos_k, seg_k):
    return (seg_q[:, None] == seg_k[None, :]) & (pos_k[None, :] <= pos_q[:, None])


def solution(mesh):
    n_cp = mesh.shape["cp"]
    next_perm = [(dev_idx, (dev_idx + 1) % n_cp) for dev_idx in range(n_cp)]

    def per_device(x_loc, seg_loc, w_q, w_k, w_v, w_o):
        cp_rank = lax.axis_index("cp")
        x_rows = lax.all_gather(x_loc, "tp", axis=0, tiled=True)
        seg_rows = lax.all_gather(seg_loc, "tp", axis=0, tiled=True)
        n_rows = x_rows.shape[0]
        piece_len = n_rows // 2
        kv_loc = w_k.shape[1]
        head_dim = w_k.shape[2]
        q_per_kv = w_q.shape[1] // kv_loc
        logit_scale = head_dim ** -0.5
        q_rows = jnp.einsum("sd,dhe->she", x_rows, w_q, preferred_element_type=jnp.float32).astype(jnp.bfloat16).reshape(n_rows, kv_loc, q_per_kv, head_dim)
        k_rows = jnp.einsum("sd,dhe->she", x_rows, w_k, preferred_element_type=jnp.float32).astype(jnp.bfloat16)
        v_rows = jnp.einsum("sd,dhe->she", x_rows, w_v, preferred_element_type=jnp.float32).astype(jnp.bfloat16)
        local_idx = jnp.arange(n_rows)

        def piece_positions(owner_rank):
            return jnp.where(local_idx < piece_len, owner_rank * piece_len + local_idx, (2 * n_cp - 1 - owner_rank) * piece_len + local_idx - piece_len)

        pos_q = piece_positions(cp_rank)
        late_q = q_rows[piece_len:]
        late_pos = pos_q[piece_len:]
        late_seg = seg_rows[piece_len:]
        state_shape = (kv_loc, q_per_kv, n_rows)
        init_state = (jnp.full(state_shape, NEG_BIG, jnp.float32), jnp.zeros(state_shape, jnp.float32), jnp.zeros(state_shape + (head_dim,), jnp.float32))
        first_state = block_update(init_state, q_rows, k_rows, v_rows, visible_mask(pos_q, seg_rows, pos_q, seg_rows), logit_scale)

        def kv_step(step_idx, loop_carry):
            k_cur, v_cur, seg_cur, softmax_state = loop_carry
            k_cur = lax.ppermute(k_cur, "cp", next_perm)
            v_cur = lax.ppermute(v_cur, "cp", next_perm)
            seg_cur = lax.ppermute(seg_cur, "cp", next_perm)
            src_rank = (cp_rank - step_idx) % n_cp
            pos_k = piece_positions(src_rank)

            def from_earlier(old_state):
                return block_update(old_state, q_rows, k_cur[:piece_len], v_cur[:piece_len], visible_mask(pos_q, seg_rows, pos_k[:piece_len], seg_cur[:piece_len]), logit_scale)

            def from_later(old_state):
                m_old, l_old, acc_old = old_state
                late_state = block_update((m_old[..., piece_len:], l_old[..., piece_len:], acc_old[:, :, piece_len:]), late_q, k_cur, v_cur, visible_mask(late_pos, late_seg, pos_k, seg_cur), logit_scale)
                return (jnp.concatenate([m_old[..., :piece_len], late_state[0]], axis=-1),
                        jnp.concatenate([l_old[..., :piece_len], late_state[1]], axis=-1),
                        jnp.concatenate([acc_old[:, :, :piece_len], late_state[2]], axis=2))

            new_state = lax.cond(src_rank < cp_rank, from_earlier, from_later, softmax_state)
            return k_cur, v_cur, seg_cur, new_state

        final_carry = lax.fori_loop(1, n_cp, kv_step, (k_rows, v_rows, seg_rows, first_state))
        l_fin = final_carry[3][1]
        acc_fin = final_carry[3][2]
        attn_out = (acc_fin / l_fin[..., None]).astype(jnp.bfloat16)
        y_part = jnp.einsum("kgqe,kged->qd", attn_out, w_o.reshape(kv_loc, q_per_kv, head_dim, -1), preferred_element_type=jnp.float32)
        return lax.psum_scatter(y_part, "tp", scatter_dimension=0, tiled=True).astype(jnp.bfloat16)

    return jax.shard_map(
        per_device,
        mesh=mesh,
        in_specs=(P(("dp", "cp", "tp"), None), P(("dp", "cp", "tp")), P(None, "tp", None), P(None, "tp", None), P(None, "tp", None), P("tp", None, None)),
        out_specs=P(("dp", "cp", "tp"), None),
        check_vma=False,
    )
```

profile of v0, /device:TPU:0, one launch (start us, length us, event | category | flops | bytes accessed | tf_op | source)
XLA Modules:
  0.0 1423.3 jit_solution(16357129004660808384)
XLA Ops:
  7.3 14.8 %all-gather = s32[4,1,512]{2,1,0:T(1,128)S(1)} all-gather(s32[1,1,512]{2,1,0:T(1,128)} %bitcast.112), channel_id=1, replica_groups=mesh['dp'=2,'tp'=4,'cp'=4] {'tp'}, dimensions={0}, use_global_device_ids=true | all-gather | bytes 10240 | tf_op jit(solution)/shard_map/all_gather | solution.py:31
  29.9 269.6 %all-gather.3.cloned.1.call-done = bf16[2048,4096]{1,0:T(8,128)(2,1)} async-done(((bf16[512,4096]{1,0:T(8,128)(2,1)}), bf16[2048,4096]{1,0:T(8,128)(2,1)}) %all-gather.3.cloned.1.call-update) | async-done | bytes 16777232 | tf_op jit(solution)/shard_map/all_gather | solution.py:30
  299.5 22.8 %fusion.53 = bf16[2048,8,128]{2,0,1:T(8,128)(2,1)S(1)} fusion(bf16[4096,8,128]{2,1,0:T(8,128)(2,1)} %param.12, bf16[2048,4096]{1,0:T(8,128)(2,1)} %all-gather.3.cloned.1.call-done), kind=kOutput, calls=%fused_computation.67 | convolution fusion | flops 17181966336 | bytes 29360128 | tf_op jit(solution)/shard_map/sd,dhe->she/dot_general | solution.py:38
  328.6 48.8 %fusion.37 = (f32[2,4,2048]{2,1,0:T(4,128)S(1)}, f32[2,2048,2048,4]{2,1,3,0:T(8,128)}) fusion(pred[2048,2048]{0,1:T(8,128)(4,1)} %compare_and_fusion.2, bf16[2048,2,4,128]{3,0,2,1:T(8,128)(2,1)} %bitcast.107, bf16[2048,2,128]{2,0,1:T(8,128)(2,1)S(1)} %fusion.58), kind=kOutput, calls=%fused_computation.51 | convolution fusion | flops 8690581504 | bytes 143720448 | tf_op jit(solution)/shard_map/qkge,ske->kgqs/dot_general | solution.py:11
  377.4 42.5 %fusion.36 = f32[2,4,2048]{2,1,0:T(4,128)S(1)} fusion(f32[2,2048,2048,4]{2,1,3,0:T(8,128)} %get-tuple-element.578, f32[2,4,2048]{2,1,0:T(4,128)S(1)} %broadcast_maximum_fusion, pred[2048,2048]{0,1:T(8,128)(4,1)} %compare_and_fusion.2), kind=kLoop, calls=%fused_computation.50 | loop fusion | flops 134201344 | bytes 138543104 | tf_op jit(solution)/shard_map/reduce_sum | solution.py:17
  428.5 54.1 %fusion.49 = f32[2,4,2048,128]{3,2,1,0:T(8,128)} fusion(f32[2,2048,2048,4]{2,1,3,0:T(8,128)} %get-tuple-element.578, f32[2,4,2048]{2,1,0:T(4,128)S(1)} %broadcast_maximum_fusion, pred[2048,2048]{0,1:T(8,128)(4,1)} %compare_and_fusion.2, f32[2,4,2048]{2,1,0:T(4,128)S(1)} %get-tuple-element.575, bf16[2048,2,128]{2,0,1:T(8,128)(2,1)S(1)} %fusion.61), kind=kOutput, calls=%fused_computation.65 | convolution fusion | flops 8726249472 | bytes 147980288 | tf_op jit(solution)/shard_map/kgqs,ske->kgqe/dot_general | solution.py:16
  482.6 351.9 %while.27 = (s32[]{:T(128)}, bf16[2048,2,128]{2,0,1:T(8,128)(2,1)S(1)}, bf16[2048,2,128]{2,0,1:T(8,128)(2,1)S(1)}, s32[2048]{0:T(1024)}, f32[2,4,2048]{2,1,0:T(4...) while((s32[]{:T(128)}, ...), condition=%wide.region_9.10_spmd.clone.clone, body=%wide.region_2.9_spmd.clone.clone.sunk | while | flops 8785031168 | bytes 282102528 | solution.py:75
  485.7 23.8 %collective-permute-done.2 = s32[2048]{0:T(1024)S(1)} collective-permute-done((s32[2048]{0:T(1024)}, s32[2048]{0:T(1024)S(1)}, u32[]{:S(2)}, u32[]{:S(2)}) %collective-permute-start.2) | collective-permute-done | bytes 8224 | tf_op jit(solution)/shard_map/while/body/eval_jaxpr/ppermute | solution.py:58
  510.1 87.8 %conditional.4 = (f32[2,4,2048]{2,1,0:T(4,128)}, f32[2,4,2048]{2,1,0:T(4,128)S(1)}, f32[2,4,2048,128]{3,2,1,0:T(8,128)}) conditional(s32[]{:T(128)} %convert_element_type.61, (f32[2,4,2048]{2,1,0:T(4,128)S(1)}, s32[1024]{0:T(1024)}, s32[2048]{0:T(1024)S(1)}, s32[2048]{0:T(1024)S(1)}, s32[1024]{0:T(1024)}, ...), branch_computations={%region_3.5_spmd, %region_6.8_spmd} | conditional | flops 8785018880 | bytes 265117760 | solution.py:72
  513.2 26.3 %fusion.6 = (f32[2,4,1024]{2,1,0:T(4,128)S(1)}, f32[2,2048,1024,4]{2,1,3,0:T(8,128)}) fusion(pred[1024,2048]{0,1:T(8,128)(4,1)S(1)} %compare_and_fusion, bf16[1024,2,4,128]{3,0,2,1:T(8,128)(2,1)} %get-tuple-element.407, bf16[2048,2,128]{2,0,1:T(8,128)(2,1)S(1)} %get-tuple-element.406), kind=kOutput, calls=%fused_computation.6 | convolution fusion | flops 4345290752 | bytes 72384512 | tf_op jit(solution)/shard_map/while/body/eval_jaxpr/cond/branch_0_fun/qkge,ske->kgqs/dot_general | solution.py:11
  539.5 21.6 %fusion.5 = f32[2,4,1024]{2,1,0:T(4,128)S(1)} fusion(f32[2,2048,1024,4]{2,1,3,0:T(8,128)} %get-tuple-element.570, f32[2,4,1024]{2,1,0:T(4,128)S(1)} %slice_maximum_fusion, pred[1024,2048]{0,1:T(8,128)(4,1)S(1)} %compare_and_fusion), kind=kLoop, calls=%fused_computation.5 | loop fusion | flops 67100672 | bytes 69271552 | tf_op jit(solution)/shard_map/while/body/eval_jaxpr/cond/branch_0_fun/reduce_sum | solution.py:17
  561.8 28.9 %multiply_add_fusion = f32[2,4,1024,128]{3,2,1,0:T(8,128)} fusion(f32[2,4,2048,128]{3,2,1,0:T(8,128)} %get-tuple-element.409, f32[2,2048,1024,4]{2,1,3,0:T(8,128)} %get-tuple-element.570, f32[2,4,1024]{2,1,0:T(4,128)S(1)} %slice_maximum_fusion, pred[1024,2048]{0,1:T(8,128)(4,1)S(1)} %compare_and_fusion, f32[2,4,1024]{2,1,0:T(4,128)S(1)} %get-tuple-element.564, ...), kind=kOutput, calls=%fused_computation.11 | convolution fusion | flops 4364173312 | bytes 78708736 | tf_op jit(solution)/shard_map/while/body/eval_jaxpr/cond/branch_0_fun/kgqs,ske->kgqe/dot_general | solution.py:16
  601.1 25.5 %collective-permute-done.2 = s32[2048]{0:T(1024)S(1)} collective-permute-done((s32[2048]{0:T(1024)}, s32[2048]{0:T(1024)S(1)}, u32[]{:S(2)}, u32[]{:S(2)}) %collective-permute-start.2) | collective-permute-done | bytes 8224 | tf_op jit(solution)/shard_map/while/body/eval_jaxpr/ppermute | solution.py:58
  627.2 87.8 %conditional.4 = (f32[2,4,2048]{2,1,0:T(4,128)}, f32[2,4,2048]{2,1,0:T(4,128)S(1)}, f32[2,4,2048,128]{3,2,1,0:T(8,128)}) conditional(s32[]{:T(128)} %convert_element_type.61, (f32[2,4,2048]{2,1,0:T(4,128)S(1)}, s32[1024]{0:T(1024)}, s32[2048]{0:T(1024)S(1)}, s32[2048]{0:T(1024)S(1)}, s32[1024]{0:T(1024)}, ...), branch_computations={%region_3.5_spmd, %region_6.8_spmd} | conditional | flops 8785018880 | bytes 265117760 | solution.py:72
  630.3 26.3 %fusion.6 = (f32[2,4,1024]{2,1,0:T(4,128)S(1)}, f32[2,2048,1024,4]{2,1,3,0:T(8,128)}) fusion(pred[1024,2048]{0,1:T(8,128)(4,1)S(1)} %compare_and_fusion, bf16[1024,2,4,128]{3,0,2,1:T(8,128)(2,1)} %get-tuple-element.407, bf16[2048,2,128]{2,0,1:T(8,128)(2,1)S(1)} %get-tuple-element.406), kind=kOutput, calls=%fused_computation.6 | convolution fusion | flops 4345290752 | bytes 72384512 | tf_op jit(solution)/shard_map/while/body/eval_jaxpr/cond/branch_0_fun/qkge,ske->kgqs/dot_general | solution.py:11
  656.6 21.6 %fusion.5 = f32[2,4,1024]{2,1,0:T(4,128)S(1)} fusion(f32[2,2048,1024,4]{2,1,3,0:T(8,128)} %get-tuple-element.570, f32[2,4,1024]{2,1,0:T(4,128)S(1)} %slice_maximum_fusion, pred[1024,2048]{0,1:T(8,128)(4,1)S(1)} %compare_and_fusion), kind=kLoop, calls=%fused_computation.5 | loop fusion | flops 67100672 | bytes 69271552 | tf_op jit(solution)/shard_map/while/body/eval_jaxpr/cond/branch_0_fun/reduce_sum | solution.py:17
  678.9 28.9 %multiply_add_fusion = f32[2,4,1024,128]{3,2,1,0:T(8,128)} fusion(f32[2,4,2048,128]{3,2,1,0:T(8,128)} %get-tuple-element.409, f32[2,2048,1024,4]{2,1,3,0:T(8,128)} %get-tuple-element.570, f32[2,4,1024]{2,1,0:T(4,128)S(1)} %slice_maximum_fusion, pred[1024,2048]{0,1:T(8,128)(4,1)S(1)} %compare_and_fusion, f32[2,4,1024]{2,1,0:T(4,128)S(1)} %get-tuple-element.564, ...), kind=kOutput, calls=%fused_computation.11 | convolution fusion | flops 4364173312 | bytes 78708736 | tf_op jit(solution)/shard_map/while/body/eval_jaxpr/cond/branch_0_fun/kgqs,ske->kgqe/dot_general | solution.py:16
  718.2 25.5 %collective-permute-done.2 = s32[2048]{0:T(1024)S(1)} collective-permute-done((s32[2048]{0:T(1024)}, s32[2048]{0:T(1024)S(1)}, u32[]{:S(2)}, u32[]{:S(2)}) %collective-permute-start.2) | collective-permute-done | bytes 8224 | tf_op jit(solution)/shard_map/while/body/eval_jaxpr/ppermute | solution.py:58
  744.3 87.8 %conditional.4 = (f32[2,4,2048]{2,1,0:T(4,128)}, f32[2,4,2048]{2,1,0:T(4,128)S(1)}, f32[2,4,2048,128]{3,2,1,0:T(8,128)}) conditional(s32[]{:T(128)} %convert_element_type.61, (f32[2,4,2048]{2,1,0:T(4,128)S(1)}, s32[1024]{0:T(1024)}, s32[2048]{0:T(1024)S(1)}, s32[2048]{0:T(1024)S(1)}, s32[1024]{0:T(1024)}, ...), branch_computations={%region_3.5_spmd, %region_6.8_spmd} | conditional | flops 8785018880 | bytes 265117760 | solution.py:72
  747.4 26.3 %fusion.6 = (f32[2,4,1024]{2,1,0:T(4,128)S(1)}, f32[2,2048,1024,4]{2,1,3,0:T(8,128)}) fusion(pred[1024,2048]{0,1:T(8,128)(4,1)S(1)} %compare_and_fusion, bf16[1024,2,4,128]{3,0,2,1:T(8,128)(2,1)} %get-tuple-element.407, bf16[2048,2,128]{2,0,1:T(8,128)(2,1)S(1)} %get-tuple-element.406), kind=kOutput, calls=%fused_computation.6 | convolution fusion | flops 4345290752 | bytes 72384512 | tf_op jit(solution)/shard_map/while/body/eval_jaxpr/cond/branch_0_fun/qkge,ske->kgqs/dot_general | solution.py:11
  773.8 21.6 %fusion.5 = f32[2,4,1024]{2,1,0:T(4,128)S(1)} fusion(f32[2,2048,1024,4]{2,1,3,0:T(8,128)} %get-tuple-element.570, f32[2,4,1024]{2,1,0:T(4,128)S(1)} %slice_maximum_fusion, pred[1024,2048]{0,1:T(8,128)(4,1)S(1)} %compare_and_fusion), kind=kLoop, calls=%fused_computation.5 | loop fusion | flops 67100672 | bytes 69271552 | tf_op jit(solution)/shard_map/while/body/eval_jaxpr/cond/branch_0_fun/reduce_sum | solution.py:17
  796.0 28.9 %multiply_add_fusion = f32[2,4,1024,128]{3,2,1,0:T(8,128)} fusion(f32[2,4,2048,128]{3,2,1,0:T(8,128)} %get-tuple-element.409, f32[2,2048,1024,4]{2,1,3,0:T(8,128)} %get-tuple-element.570, f32[2,4,1024]{2,1,0:T(4,128)S(1)} %slice_maximum_fusion, pred[1024,2048]{0,1:T(8,128)(4,1)S(1)} %compare_and_fusion, f32[2,4,1024]{2,1,0:T(4,128)S(1)} %get-tuple-element.564, ...), kind=kOutput, calls=%fused_computation.11 | convolution fusion | flops 4364173312 | bytes 78708736 | tf_op jit(solution)/shard_map/while/body/eval_jaxpr/cond/branch_0_fun/kgqs,ske->kgqe/dot_general | solution.py:16
  834.5 29.2 %convolution_bitcast_fusion = f32[2048,4096]{1,0:T(8,128)} fusion(bf16[2,4,128,4096]{3,2,1,0:T(8,128)(2,1)} %bitcast.113, f32[2,4,2048,128]{3,2,1,0:T(8,128)} %get-tuple-element.444, f32[2,4,2048]{2,1,0:T(4,128)S(1)} %get-tuple-element.445), kind=kOutput, calls=%fused_computation.54 | convolution fusion | flops 17184063488 | bytes 50397184 | tf_op jit(solution)/shard_map/kgqe,kged->qd/dot_general | solution.py:79
  863.8 546.5 %reduce-scatter.2.cloned.1.call-done = f32[512,4096]{1,0:T(8,128)} async-done(((f32[2048,4096]{1,0:T(8,128)}), f32[512,4096]{1,0:T(8,128)}) %reduce-scatter.2.cloned.1.call-update) | async-done | bytes 8388624 | tf_op jit(solution)/shard_map/reduce_scatter | solution.py:80
  (102 shorter events, 75.2 us)
Async XLA Ops:
  6.5 317.3 %copy-start = (bf16[4096,2,128]{2,1,0:T(2,128)(2,1)S(1)}, bf16[4096,2,128]{2,1,0:T(2,128)(2,1)}, u32[]{:S(2)}) copy-start(bf16[4096,2,128]{2,1,0:T(2,128)(2,1)} %param.13) | copy-start | bytes 6291460
  6.5 292.9 %all-gather.3.cloned.1.call-start = ((), (), s32[]{:S(2)}) async-start(), calls=%async_computation.1 | async-start | bytes 20971520 | tf_op jit(solution)/shard_map/all_gather | solution.py:30
  7.3 1403.0 %reduce-scatter.2.cloned.1.call-start = ((), (), s32[]{:S(2)}) async-start(), calls=%async_computation.2 | async-start | bytes 41943040 | tf_op jit(solution)/shard_map/reduce_scatter | solution.py:80
  22.1 300.2 %copy-start.4 = (s32[4,1,512]{2,1,0:T(1,128)}, s32[4,1,512]{2,1,0:T(1,128)S(1)}, u32[]{:S(2)}) copy-start(s32[4,1,512]{2,1,0:T(1,128)S(1)} %all-gather) | copy-start | bytes 24580
  299.5 24.4 %copy-start.6 = (bf16[2048,4096]{1,0:T(8,128)(2,1)S(1)}, bf16[2048,4096]{1,0:T(8,128)(2,1)}, u32[]{:S(2)}) copy-start(bf16[2048,4096]{1,0:T(8,128)(2,1)} %all-gather.3.cloned.1.call-done) | copy-start | bytes 50331652
  322.3 6.3 copy-start.3
  328.5 48.8 %copy-start.8 = (bf16[2048,2,128]{2,0,1:T(8,128)(2,1)}, bf16[2048,2,128]{2,0,1:T(8,128)(2,1)S(1)}, u32[]{:S(2)}) copy-start(bf16[2048,2,128]{2,0,1:T(8,128)(2,1)S(1)} %fusion.58) | copy-start | bytes 3145732
  377.4 42.6 %copy-start.7 = (bf16[4096,2,128]{2,1,0:T(2,128)(2,1)S(1)}, bf16[4096,2,128]{2,1,0:T(2,128)(2,1)}, u32[]{:S(2)}) copy-start(bf16[4096,2,128]{2,1,0:T(2,128)(2,1)} %param.14) | copy-start | bytes 6291460
  428.5 54.1 %copy-start.5 = (s32[4,1,512]{2,1,0:T(1,128)S(1)}, s32[4,1,512]{2,1,0:T(1,128)}, u32[]{:S(2)}) copy-start(s32[4,1,512]{2,1,0:T(1,128)} %copy-done.4) | copy-start | bytes 24580
  428.5 54.1 %copy-start.9 = (bf16[2048,2,128]{2,0,1:T(8,128)(2,1)S(1)}, bf16[2048,2,128]{2,0,1:T(8,128)(2,1)}, u32[]{:S(2)}) copy-start(bf16[2048,2,128]{2,0,1:T(8,128)(2,1)} %copy-done.8) | copy-start | bytes 3145732
  483.0 1.0 copy-start.10
  483.9 26.1 %collective-permute-start = (bf16[2048,2,128]{2,0,1:T(8,128)(2,1)S(1)}, bf16[2048,2,128]{2,0,1:T(8,128)(2,1)S(1)}, u32[]{:S(2)}, u32[]{:S(2)}) collective-permute-start(bf16[2048,2,128]{2,0,1:T(8,128)(2,1)S(1)} %get-tuple-element.707), channel_id=1, source_target_pairs={{0,1},{1,2},{2,3},{3,0},{4,5},{5,6},{6,7},{7,4},{8,9},{9,10},{10,1... | collective-permute-start | bytes 3145736 | tf_op jit(solution)/shard_map/while/body/eval_jaxpr/ppermute | solution.py:56
  484.1 26.0 %collective-permute-start.1 = (bf16[2048,2,128]{2,0,1:T(8,128)(2,1)}, bf16[2048,2,128]{2,0,1:T(8,128)(2,1)}, u32[]{:S(2)}, u32[]{:S(2)}) collective-permute-start(bf16[2048,2,128]{2,0,1:T(8,128)(2,1)} %copy-done.10), channel_id=1, source_target_pairs={{0,1},{1,2},{2,3},{3,0},{4,5},{5,6},{6,7},{7,4},{8,9},{9,10},{10,1... | collective-permute-start | bytes 3145736 | tf_op jit(solution)/shard_map/while/body/eval_jaxpr/ppermute | solution.py:57
  485.5 23.9 %collective-permute-start.2 = (s32[2048]{0:T(1024)}, s32[2048]{0:T(1024)S(1)}, u32[]{:S(2)}, u32[]{:S(2)}) collective-permute-start(s32[2048]{0:T(1024)} %get-tuple-element.709), channel_id=1, source_target_pairs={{0,1},{1,2},{2,3},{3,0},{4,5},{5,6},{6,7},{7,4},{8,9},{9,10},{10,1... | collective-permute-start | bytes 24584 | tf_op jit(solution)/shard_map/while/body/eval_jaxpr/ppermute | solution.py:58
  590.7 3.4 copy-start.2
  601.1 26.1 %collective-permute-start = (bf16[2048,2,128]{2,0,1:T(8,128)(2,1)S(1)}, bf16[2048,2,128]{2,0,1:T(8,128)(2,1)S(1)}, u32[]{:S(2)}, u32[]{:S(2)}) collective-permute-start(bf16[2048,2,128]{2,0,1:T(8,128)(2,1)S(1)} %get-tuple-element.707), channel_id=1, source_target_pairs={{0,1},{1,2},{2,3},{3,0},{4,5},{5,6},{6,7},{7,4},{8,9},{9,10},{10,1... | collective-permute-start | bytes 3145736 | tf_op jit(solution)/shard_map/while/body/eval_jaxpr/ppermute | solution.py:56
  601.1 26.1 %collective-permute-start.1 = (bf16[2048,2,128]{2,0,1:T(8,128)(2,1)}, bf16[2048,2,128]{2,0,1:T(8,128)(2,1)}, u32[]{:S(2)}, u32[]{:S(2)}) collective-permute-start(bf16[2048,2,128]{2,0,1:T(8,128)(2,1)} %copy-done.10), channel_id=1, source_target_pairs={{0,1},{1,2},{2,3},{3,0},{4,5},{5,6},{6,7},{7,4},{8,9},{9,10},{10,1... | collective-permute-start | bytes 3145736 | tf_op jit(solution)/shard_map/while/body/eval_jaxpr/ppermute | solution.py:57
  601.1 25.5 %collective-permute-start.2 = (s32[2048]{0:T(1024)}, s32[2048]{0:T(1024)S(1)}, u32[]{:S(2)}, u32[]{:S(2)}) collective-permute-start(s32[2048]{0:T(1024)} %get-tuple-element.709), channel_id=1, source_target_pairs={{0,1},{1,2},{2,3},{3,0},{4,5},{5,6},{6,7},{7,4},{8,9},{9,10},{10,1... | collective-permute-start | bytes 24584 | tf_op jit(solution)/shard_map/while/body/eval_jaxpr/ppermute | solution.py:58
  707.8 3.4 copy-start.2
  718.2 26.1 %collective-permute-start = (bf16[2048,2,128]{2,0,1:T(8,128)(2,1)S(1)}, bf16[2048,2,128]{2,0,1:T(8,128)(2,1)S(1)}, u32[]{:S(2)}, u32[]{:S(2)}) collective-permute-start(bf16[2048,2,128]{2,0,1:T(8,128)(2,1)S(1)} %get-tuple-element.707), channel_id=1, source_target_pairs={{0,1},{1,2},{2,3},{3,0},{4,5},{5,6},{6,7},{7,4},{8,9},{9,10},{10,1... | collective-permute-start | bytes 3145736 | tf_op jit(solution)/shard_map/while/body/eval_jaxpr/ppermute | solution.py:56
  718.2 26.1 %collective-permute-start.1 = (bf16[2048,2,128]{2,0,1:T(8,128)(2,1)}, bf16[2048,2,128]{2,0,1:T(8,128)(2,1)}, u32[]{:S(2)}, u32[]{:S(2)}) collective-permute-start(bf16[2048,2,128]{2,0,1:T(8,128)(2,1)} %copy-done.10), channel_id=1, source_target_pairs={{0,1},{1,2},{2,3},{3,0},{4,5},{5,6},{6,7},{7,4},{8,9},{9,10},{10,1... | collective-permute-start | bytes 3145736 | tf_op jit(solution)/shard_map/while/body/eval_jaxpr/ppermute | solution.py:57
  718.2 25.5 %collective-permute-start.2 = (s32[2048]{0:T(1024)}, s32[2048]{0:T(1024)S(1)}, u32[]{:S(2)}, u32[]{:S(2)}) collective-permute-start(s32[2048]{0:T(1024)} %get-tuple-element.709), channel_id=1, source_target_pairs={{0,1},{1,2},{2,3},{3,0},{4,5},{5,6},{6,7},{7,4},{8,9},{9,10},{10,1... | collective-permute-start | bytes 24584 | tf_op jit(solution)/shard_map/while/body/eval_jaxpr/ppermute | solution.py:58
  824.9 3.4 copy-start.2
  863.7 552.6 %copy-start.1 = (bf16[4096,2,128]{2,1,0:T(2,128)(2,1)S(1)}, bf16[4096,2,128]{2,1,0:T(2,128)(2,1)}, u32[]{:S(2)}) copy-start(bf16[4096,2,128]{2,1,0:T(2,128)(2,1)} %param.13) | copy-start | bytes 6291460
  (2 other events, 1.9 us)
Sparse Core Ops, SparseCore 0:
  8.9 290.5 all-gather.2
  863.9 546.3 reduce-scatter.1
where the time goes:
time: 1440 us; the launch traced here: 1420 us
  waiting for transfers between devices  892 us (62%)
  matrix products  334 us (23%)
  other arithmetic  142 us (10%)
  local copies, waits for them, and re-layouts  24.8 us (2%)
  blocking collectives  14.8 us (1%)
    reduce_scatter x1, waiting for transfers between devices, per_device(): lax.psum_scatter(y_part, 'tp', scatter_dimension=0, tiled=True)  547 us
    all_gather x1, waiting for transfers between devices, per_device(): x_rows = lax.all_gather(x_loc, 'tp', axis=0, tiled=True)  270 us
    dot_general x4, matrix products, block_update(): jnp.einsum('kgqs,ske->kgqe', prob_blk.astype(jnp.bfloat16), v_blk, prefer...  141 us
    dot_general x4, matrix products, block_update(): jnp.einsum('qkge,ske->kgqs', q_blk, k_blk, preferred_element_type=jnp.flo...  128 us
    reduce_sum x4, other arithmetic, block_update(): jnp.sum(prob_blk, axis=-1)  107 us
    ppermute x3, waiting for transfers between devices, kv_step(): seg_cur = lax.ppermute(seg_cur, 'cp', next_perm)  74.8 us
    dot_general x1, matrix products, per_device(): jnp.einsum('kgqe,kged->qd', attn_out, w_o.reshape(kv_loc, q_per_kv, head_...  29.2 us
  transfers between devices with their start and end apart: 11, of which 5 were waited for; matrix products, arithmetic and copies ran while one was open for 1% of the time, Pallas kernels for 0%

commit v1 on v0

v1 whole, which is shorter than its diff:
```python
import functools
import math

import jax
import jax.numpy as jnp
from jax import lax
from jax.experimental import pallas as pl
from jax.experimental.pallas import tpu as pltpu
from jax.sharding import PartitionSpec as P


NEG_BIG = -1e30
K_TILE = 512
HALVES = 2


def flash_kernel(n_cp, n_tp, group, exp_scale, bounds_ref, q_ref, *refs):
    k_refs, v_refs = refs[:HALVES], refs[HALVES:2 * HALVES]
    start_ref, o_ref, q_all, m_ref, l_ref, acc_ref = refs[2 * HALVES:]
    tile = pl.program_id(0)
    head_dim = q_all.shape[1]
    rows = q_ref.shape[0]
    per_piece = n_tp // 2
    sub = K_TILE // HALVES
    for head in range(group):
        q_all[pl.ds(head * rows, rows), :] = q_ref[:, head * head_dim:(head + 1) * head_dim]
    m_ref[...] = jnp.full_like(m_ref, NEG_BIG)
    l_ref[...] = jnp.zeros_like(l_ref)
    acc_ref[...] = jnp.zeros_like(acc_ref)
    first_pos = bounds_ref[0, tile]
    cp_rank = bounds_ref[5, 0]

    def step(masked, blk, carry):
        piece = blk // per_piece
        early = piece < n_cp
        owner = jnp.where(early, piece, 2 * n_cp - 1 - piece)
        slot = jnp.bitwise_xor(owner, cp_rank)
        part = blk % per_piece + jnp.where(early, 0, per_piece)
        off = pl.multiple_of((slot * n_tp + part) * sub, sub)
        k_blk = jnp.concatenate([ref[pl.ds(off, sub), :] for ref in k_refs], axis=0)
        v_blk = jnp.concatenate([ref[pl.ds(off, sub), :] for ref in v_refs], axis=0)
        scores = lax.dot_general(q_all[...], k_blk, (((1,), (1,)), ((), ())), preferred_element_type=jnp.float32) * exp_scale
        if masked:
            key_pos = blk * K_TILE + lax.broadcasted_iota(jnp.int32, (rows, K_TILE), 1)
            row_pos = first_pos + lax.broadcasted_iota(jnp.int32, (rows, K_TILE), 0)
            allowed = (key_pos >= start_ref[...]) & (key_pos <= row_pos)
            scores = jnp.where(allowed[None], scores.reshape(group, rows, K_TILE), NEG_BIG).reshape(group * rows, K_TILE)
        m_old = m_ref[...]
        m_new = jnp.maximum(m_old, jnp.max(scores, axis=1, keepdims=True))
        probs = [jnp.exp2(scores[:, j:j + head_dim] - m_new) for j in range(0, K_TILE, head_dim)]
        rescale = jnp.exp2(m_old - m_new)
        l_ref[...] = rescale * l_ref[...] + functools.reduce(jnp.add, probs)
        prob_blk = jnp.concatenate([prob.astype(jnp.bfloat16) for prob in probs], axis=1)
        acc_ref[...] = rescale * acc_ref[...] + jnp.dot(prob_blk, v_blk, preferred_element_type=jnp.float32)
        m_ref[...] = m_new
        return carry

    lo = bounds_ref[1, tile]
    mid = bounds_ref[2, tile]
    full_end = bounds_ref[3, tile]
    hi = bounds_ref[4, tile]
    lax.fori_loop(lo, mid, functools.partial(step, True), 0)
    lax.fori_loop(mid, full_end, functools.partial(step, False), 0)
    lax.fori_loop(full_end, hi, functools.partial(step, True), 0)
    out = acc_ref[...] / jnp.sum(l_ref[...], axis=1, keepdims=True)
    for head in range(group):
        o_ref[:, head * head_dim:(head + 1) * head_dim] = out[head * rows:(head + 1) * rows].astype(o_ref.dtype)


def flash(n_cp, n_tp, q_rows, kv_halves, kv_idx, kv_loc, head_dim, bounds, row_start):
    n_rows = q_rows.shape[0]
    tile = n_rows // n_tp
    group = q_rows.shape[1] // (kv_loc * head_dim)
    exp_scale = head_dim ** -0.5 * math.log2(math.e)
    stacked = group * tile
    n_keys = kv_halves[0].shape[0]
    grid_spec = pltpu.PrefetchScalarGridSpec(
        num_scalar_prefetch=1,
        grid=(n_tp,),
        in_specs=[pl.BlockSpec((tile, group * head_dim), lambda i, b: (i, kv_idx))]
        + [pl.BlockSpec((n_keys, head_dim), lambda i, b: (0, kv_idx))] * HALVES
        + [pl.BlockSpec((n_keys, head_dim), lambda i, b: (0, kv_loc + kv_idx))] * HALVES
        + [pl.BlockSpec((tile, 1), lambda i, b: (i, 0))],
        out_specs=pl.BlockSpec((tile, group * head_dim), lambda i, b: (i, 0)),
        scratch_shapes=[
            pltpu.VMEM((stacked, head_dim), jnp.bfloat16),
            pltpu.VMEM((stacked, head_dim), jnp.float32),
            pltpu.VMEM((stacked, head_dim), jnp.float32),
            pltpu.VMEM((stacked, head_dim), jnp.float32),
        ],
    )
    n_scores = n_rows * n_keys * HALVES // 4 * group
    return pl.pallas_call(
        functools.partial(flash_kernel, n_cp, n_tp, group, exp_scale),
        grid_spec=grid_spec,
        out_shape=jax.ShapeDtypeStruct((n_rows, group * head_dim), jnp.bfloat16),
        compiler_params=pltpu.CompilerParams(dimension_semantics=("arbitrary",), vmem_limit_bytes=48 << 20),
        cost_estimate=pl.CostEstimate(flops=4 * n_scores * head_dim, bytes_accessed=12 << 20, transcendentals=n_scores),
    )(bounds, q_rows, *kv_halves, *kv_halves, row_start)


def project_kernel(n_tp, heads, n_o, n_w, rank_ref, *refs):
    o_refs, w_refs = refs[:n_o], refs[n_o:n_o + n_w]
    y_ref, o_full = refs[-2:]
    n_cols = y_ref.shape[-1]
    head_dim = w_refs[0].shape[1]
    sub = o_refs[0].shape[0]
    n_kv = n_o // (HALVES * n_tp)

    @pl.when(pl.program_id(0) == 0)
    def _():
        for half in range(HALVES):
            for kv_idx in range(n_kv):
                for bit in range(n_tp):
                    piece = o_refs[(half * n_kv + kv_idx) * n_tp + bit]
                    source = jnp.bitwise_xor(rank_ref[0], bit)
                    for head in range(heads):
                        part = jnp.bitwise_xor(rank_ref[1], kv_idx * heads + head)
                        col = pl.multiple_of((part * n_tp + source) * head_dim, head_dim)
                        o_full[half * sub:(half + 1) * sub, pl.ds(col, head_dim)] = piece[:, head * head_dim:(head + 1) * head_dim]

    total = None
    start = 0
    for w_ref in w_refs:
        depth = w_ref.shape[0] * head_dim
        term = jnp.dot(o_full[:, start:start + depth], w_ref[...].reshape(depth, n_cols), preferred_element_type=jnp.float32)
        total = term if total is None else total + term
        start += depth
    y_ref[...] = total.astype(y_ref.dtype)


def project(ranks, n_tp, pieces, w_parts, heads, d_model, y_left=None, n_cols=512):
    head_dim, cols = w_parts[0].shape[1:]
    sub, piece_cols = pieces[0].shape
    rows = HALVES * sub
    depth = sum(part.shape[0] for part in w_parts) * head_dim
    first = 0 if y_left is None else cols // n_cols
    extra = [] if y_left is None else [y_left]
    grid_spec = pltpu.PrefetchScalarGridSpec(
        num_scalar_prefetch=1,
        grid=(cols // n_cols,),
        in_specs=[pl.BlockSpec((sub, piece_cols), lambda i, t: (0, 0))] * len(pieces)
        + [pl.BlockSpec((part.shape[0], head_dim, n_cols), lambda i, t: (0, 0, i)) for part in w_parts]
        + [pl.BlockSpec(memory_space=pl.ANY)] * len(extra),
        out_specs=pl.BlockSpec((rows, n_cols), lambda i, t: (0, first + i)),
        scratch_shapes=[pltpu.VMEM((rows, depth), jnp.bfloat16)],
    )
    return pl.pallas_call(
        functools.partial(project_kernel, n_tp, heads, len(pieces), len(w_parts)),
        grid_spec=grid_spec,
        out_shape=jax.ShapeDtypeStruct((rows, d_model), jnp.bfloat16),
        input_output_aliases={1 + len(pieces) + len(w_parts): 0} if extra else {},
        compiler_params=pltpu.CompilerParams(dimension_semantics=("arbitrary",), vmem_limit_bytes=48 << 20),
        cost_estimate=pl.CostEstimate(flops=2 * rows * depth * cols, bytes_accessed=24 << 20, transcendentals=0),
    )(ranks, *pieces, *w_parts, *extra)


def solution(mesh):
    n_cp = mesh.shape["cp"]
    n_tp = mesh.shape["tp"]
    n_dp = mesh.shape["dp"]

    def swap(arr, axis, bit):
        return lax.ppermute(arr, axis, [(src, src ^ bit) for src in range(mesh.shape[axis])])

    def per_device(x_loc, seg_loc, w_q, w_k, w_v, w_o):
        cp_rank = lax.axis_index("cp")
        tp_rank = lax.axis_index("tp")
        own_rows, d_model = x_loc.shape
        kv_loc = w_k.shape[1]
        head_dim = w_k.shape[2]
        n_rows = own_rows * n_tp
        piece_len = n_rows // 2
        width = w_q.shape[1] * head_dim
        sub = own_rows // HALVES

        part_rows = w_o.shape[0] * head_dim // (n_dp * n_cp)
        part_idx = lax.axis_index("dp") * n_cp + cp_rank
        w_o_part = lax.dynamic_slice_in_dim(w_o.reshape(width, d_model), part_idx * part_rows, part_rows)
        half_cols = d_model // 2
        mid_tp = n_tp // 2

        def gather_wo(side):
            w_tp = lax.all_gather(w_o_part[:, side * half_cols:(side + 1) * half_cols], "tp", axis=0)
            w_dp = swap(w_tp, "dp", 1)
            w_cp = swap(w_tp, "cp", 2)
            w_diag0 = swap(w_dp[:mid_tp], "cp", 2)
            w_diag1 = swap(w_cp[mid_tp:], "dp", 1)
            near = [w_tp, w_cp, w_dp, w_diag0, w_diag1]
            far = []
            for part in near:
                far.append(swap(part, "cp", 1))
            return [near[0], far[0], near[1], far[1], near[2], far[2], near[3], near[4], far[3], far[4]]

        x_halves = []
        for half in range(HALVES):
            x_halves.append(lax.all_gather(x_loc[half * sub:(half + 1) * sub], "tp", axis=0, tiled=True))
        w_sides = [gather_wo(side) for side in range(2)]
        seg_all = lax.all_gather(seg_loc, ("cp", "tp"), axis=0, tiled=True)
        w_q2 = w_q.reshape(d_model, width)
        w_kv = jnp.concatenate([w_k.reshape(d_model, -1), w_v.reshape(d_model, -1)], axis=1)

        seg_rows = lax.dynamic_slice_in_dim(seg_all, cp_rank * n_rows, n_rows)
        row_start = jnp.sum((seg_all[None, :] < seg_rows[:, None]).astype(jnp.int32), axis=1)
        tiles = n_rows // sub
        tile_row = jnp.arange(tiles) * sub
        first_pos = jnp.where(tile_row < piece_len, cp_rank * piece_len + tile_row, (2 * n_cp - 1 - cp_rank) * piece_len + tile_row - piece_len)
        start_tiles = row_start.reshape(tiles, sub)
        lo = start_tiles[:, 0] // K_TILE
        full_end = (first_pos + 1) // K_TILE
        mid = jnp.minimum(jnp.maximum((start_tiles[:, -1] + K_TILE - 1) // K_TILE, lo), full_end)
        hi = (first_pos + sub - 1) // K_TILE + 1
        bounds = jnp.stack([first_pos, lo, mid, full_end, hi, jnp.full_like(lo, cp_rank)]).astype(jnp.int32)
        bounds = bounds.reshape(-1, n_tp, HALVES)
        row_start = row_start.reshape(n_tp, HALVES, sub)
        x_halves[0], w_q2, w_kv, bounds, row_start = lax.optimization_barrier((x_halves[0], w_q2, w_kv, bounds, row_start))

        q_halves, kv_halves = [], []
        for x_half in x_halves:
            kv_own = jnp.dot(x_half, w_kv, preferred_element_type=jnp.float32).astype(jnp.bfloat16)
            kv_far = swap(kv_own, "cp", 2)
            kv_chip = swap(kv_own, "cp", 1)
            kv_diag = swap(kv_far, "cp", 1)
            kv_halves.append(jnp.concatenate([kv_own, kv_chip, kv_far, kv_diag], axis=0))
            q_halves.append(jnp.dot(x_half, w_q2, preferred_element_type=jnp.float32).astype(jnp.bfloat16))

        pieces = []
        for half in range(HALVES):
            for kv_idx in range(kv_loc):
                o_rows = flash(n_cp, n_tp, q_halves[half], kv_halves, kv_idx, kv_loc, head_dim, bounds[:, :, half], row_start[:, half].reshape(-1, 1))
                o_tiles = o_rows.reshape(n_tp, sub, -1)
                for bit in range(n_tp):
                    mine = lax.dynamic_index_in_dim(o_tiles, tp_rank ^ bit, 0, False)
                    pieces.append(swap(mine, "tp", bit) if bit else mine)
        ranks = jnp.stack([tp_rank, part_idx]).astype(jnp.int32)
        y_left = project(ranks, n_tp, pieces, w_sides[0], w_q.shape[1] // kv_loc, d_model)
        return project(ranks, n_tp, pieces, w_sides[1], w_q.shape[1] // kv_loc, d_model, y_left)


    return jax.shard_map(
        per_device,
        mesh=mesh,
        in_specs=(P(("dp", "cp", "tp"), None), P(("dp", "cp", "tp")), P(None, "tp", None), P(None, "tp", None), P(None, "tp", None), P("tp", None, None)),
        out_specs=P(("dp", "cp", "tp"), None),
        check_vma=False,
    )
```

time: 1440 us -> 707 us (0.49)
  waiting for transfers between devices: 892 us -> 384 us
  matrix products: 334 us -> 37.9 us
  Pallas kernels: 0 us -> 132 us
  other arithmetic: 142 us -> 19.3 us
  starting transfers between devices: 1.76 us -> 42.1 us
  blocking collectives: 14.8 us -> 36.1 us
    reduce_scatter x1 -> x0, waiting for transfers between devices: 547 us -> none  [per_device(): lax.psum_scatter(y_part, 'tp', scatter_dimension=0, tiled=True)]
    dot_general x12 -> x4, matrix products: 334 us -> 37.9 us  [the longest x2 22.2 us: per_device(): jnp.dot(x_half, w_q2, preferred_element_type=jnp.float32)]
    pallas_call x0 -> x6, Pallas kernels: none -> 132 us  [the longest x4 103 us: flash(): pl.pallas_call(functools.partial(flash_kernel, n_cp, n_tp, group, exp_sca...]
    reduce_sum x4 -> x1, other arithmetic: 107 us -> 9.36 us  [per_device(): jnp.sum((seg_all[None, :] < seg_rows[:, None]).astype(jnp.int32), axis=1)]
    ppermute x9 -> x36, starting transfers between devices: 1.72 us -> 41.9 us  [swap(): lax.ppermute(arr, axis, [(src, src ^ bit) for src in range(mesh.shape[axi...]
    all_gather x1, blocking collectives: 14.8 us -> 36.1 us  [per_device(): seg_all = lax.all_gather(seg_loc, ('cp', 'tp'), axis=0, tiled=True)]
    ppermute x9 -> x36, waiting for transfers between devices: 74.8 us -> 94.3 us  [swap(): lax.ppermute(arr, axis, [(src, src ^ bit) for src in range(mesh.shape[axi...]
    all_gather x1 -> x4, waiting for transfers between devices: 270 us -> 288 us  [the longest x2 247 us: per_device(): lax.all_gather(x_loc[half * sub:(half + 1) * sub], 'tp', axis=0, tiled=True)]
  transfers between devices with their start and end apart: 11 -> 40, of which waited for: 5 -> 13; matrix products, arithmetic and copies ran while one was open for 1% -> 12% of each run, Pallas kernels for 0% -> 17%
where the time goes in v1:
time: 707 us; the launch traced here: 697 us
  waiting for transfers between devices  384 us (54%)
  Pallas kernels  132 us (19%)
  starting transfers between devices  42.1 us (6%)
  matrix products  37.9 us (5%)
  blocking collectives  36.1 us (5%)
  local copies, waits for them, and re-layouts  32.7 us (5%)
  other arithmetic  19.3 us (3%)
  between operations  13.8 us (2%)
    all_gather x2, waiting for transfers between devices, per_device(): lax.all_gather(x_loc[half * sub:(half + 1) * sub], 'tp', axis=0, tiled=True)  247 us
    pallas_call x4, Pallas kernels, flash(): pl.pallas_call(functools.partial(flash_kernel, n_cp, n_tp, group, exp_sca...  103 us
    ppermute x36, waiting for transfers between devices, swap(): lax.ppermute(arr, axis, [(src, src ^ bit) for src in range(mesh.shape[axi...  94.3 us
    ppermute x36, starting transfers between devices, swap(): lax.ppermute(arr, axis, [(src, src ^ bit) for src in range(mesh.shape[axi...  41.9 us
    all_gather x2, waiting for transfers between devices, gather_wo(): lax.all_gather(w_o_part[:, side * half_cols:(side + 1) * half_cols], 'tp'...  41.6 us
    all_gather x1, blocking collectives, per_device(): seg_all = lax.all_gather(seg_loc, ('cp', 'tp'), axis=0, tiled=True)  36.1 us
    pallas_call x2, Pallas kernels, project(): pl.pallas_call(functools.partial(project_kernel, n_tp, heads, len(pieces)...  28.5 us
    dot_general x2, matrix products, per_device(): jnp.dot(x_half, w_q2, preferred_element_type=jnp.float32)  22.2 us
  transfers between devices with their start and end apart: 40, of which 13 were waited for; matrix products, arithmetic and copies ran while one was open for 12% of the time, Pallas kernels for 17%

profile of v1, /device:TPU:0, one launch (start us, length us, event | category | flops | bytes accessed | tf_op | source)
XLA Modules:
  0.0 697.4 jit_solution(11016584074137979970)
XLA Ops:
  15.0 36.1 %all-gather.2 = s32[16,1,512]{2,1,0:T(1,128)S(1)} all-gather(s32[1,1,512]{2,1,0:T(1,128)S(1)} %bitcast.87), channel_id=1, replica_groups=mesh['dp'=2,'tp'=4,'cp'=4] {'cp','tp'}, dimensions={0}, use_global_device_ids=true | all-gather | bytes 34816 | tf_op jit(solution)/shard_map/all_gather | solution.py:199
  51.1 9.4 %convert_reduce_fusion = s32[2048]{0:T(1024)S(1)} fusion(s32[8192]{0:T(1024)S(1)} %bitcast.84, s32[2048]{0:T(1024)S(1)} %dynamic_slice.55), kind=kLoop, calls=%fused_computation | loop fusion | flops 50329600 | bytes 49152 | tf_op jit(solution)/shard_map/reduce_sum | solution.py:204
  62.5 41.6 %all-gather.12.cloned.1.call-done = bf16[512,2048]{1,0:T(8,128)(2,1)} async-done(((bf16[128,2048]{1,0:T(8,128)(2,1)}), bf16[512,2048]{1,0:T(8,128)(2,1)}) %all-gather.12.cloned.1.call-update) | async-done | bytes 2097168 | tf_op jit(solution)/shard_map/all_gather | solution.py:184
  108.0 9.5 %copy.66 = bf16[512,8,8,128]{3,1,2,0:T(8,128)(2,1)} copy(bf16[512,8,8,128]{3,2,1,0:T(8,128)(2,1)} %bitcast.75) | data formatting | bytes 16777216
  127.6 24.0 %collective-permute-done.21.refs_20_ = bf16[4,128,2048]{2,1,0:T(8,128)(2,1)} collective-permute-done((bf16[4,128,2048]{2,1,0:T(8,128)(2,1)}, bf16[4,128,2048]{2,1,0:T(8,128)(2,1)}, u32[]{:S(2)}, u32[]{:S(2)}) %collective-permute-start.21) | collective-permute-done | bytes 2097184 | tf_op jit(solution)/shard_map/ppermute | solution.py:164
  156.7 97.4 %all-gather.8.cloned.1.call-done = bf16[1024,4096]{1,0:T(8,128)(2,1)} async-done(((bf16[256,4096]{1,0:T(8,128)(2,1)}), bf16[1024,4096]{1,0:T(8,128)(2,1)}) %all-gather.8.cloned.1.call-update) | async-done | bytes 8388624 | tf_op jit(solution)/shard_map/all_gather | solution.py:197
  254.1 149.3 %all-gather.10.cloned.1.call-done = bf16[1024,4096]{1,0:T(8,128)(2,1)} async-done(((bf16[256,4096]{1,0:T(8,128)(2,1)}), bf16[1024,4096]{1,0:T(8,128)(2,1)}) %all-gather.10.cloned.1.call-update) | async-done | bytes 8388624 | tf_op jit(solution)/shard_map/all_gather | solution.py:197
  403.4 10.2 %fusion = bf16[1024,512]{1,0:T(8,128)(2,1)} fusion(bf16[1024,4096]{1,0:T(8,128)(2,1)} %all-gather.10.cloned.1.call-done, bf16[4096,512]{1,0:T(8,128)(2,1)} %pad_maximum_fusion), kind=kOutput, calls=%fused_computation.11 | convolution fusion | flops 4295491584 | bytes 13631488 | tf_op jit(solution)/shard_map/dot_general | solution.py:220
  415.1 5.5 convolution_convert_fusion.2
  421.1 12.1 %convolution_convert_fusion.q_ref = bf16[1024,1024]{1,0:T(8,128)(2,1)S(1)} fusion(bf16[1024,4096]{1,0:T(8,128)(2,1)S(1)} %copy-done.5, bf16[4096,1024]{1,0:T(8,128)(2,1)} %bitcast.76), kind=kOutput, calls=%fused_computation.8 | convolution fusion | flops 8590983168 | bytes 18874368 | tf_op jit(solution)/shard_map/dot_general | solution.py:225
  433.4 6.5 collective-permute-done.4
  439.9 21.5 %collective-permute-done.1 = bf16[1024,512]{1,0:T(8,128)(2,1)} collective-permute-done((bf16[1024,512]{1,0:T(8,128)(2,1)}, bf16[1024,512]{1,0:T(8,128)(2,1)}, u32[]{:S(2)}, u32[]{:S(2)}) %collective-permute-start.1) | collective-permute-done | bytes 1048608 | tf_op jit(solution)/shard_map/ppermute | solution.py:164
  461.5 10.1 %convert_bitcast_fusion.q_ref = bf16[1024,1024]{1,0:T(8,128)(2,1)} fusion(bf16[1024,4096]{1,0:T(8,128)(2,1)S(1)} %bitcast.89, bf16[4096,1024]{1,0:T(8,128)(2,1)S(1)} %bitcast.79), kind=kOutput, calls=%fused_computation.7 | convolution fusion | flops 8590983168 | bytes 18874368 | tf_op jit(solution)/shard_map/dot_general | solution.py:225
  483.6 14.8 %collective-permute-done.33.refs_23_ = bf16[2,128,2048]{2,1,0:T(8,128)(2,1)S(1)} collective-permute-done((bf16[2,128,2048]{2,1,0:T(8,128)(2,1)}, bf16[2,128,2048]{2,1,0:T(8,128)(2,1)S(1)}, u32[]{:S(2)}, u32[]{:S(2)}) %collective-permute-start.33) | collective-permute-done | bytes 1048608 | tf_op jit(solution)/shard_map/ppermute | solution.py:164
  499.2 26.2 %shard_map.67 = bf16[1024,512]{1,0:T(8,128)(2,1)S(1)} custom-call(s32[6,4]{1,0:T(8,128)S(1)} %copy.54.bounds_ref, bf16[1024,1024]{1,0:T(8,128)(2,1)S(1)} %copy-done, bf16[4096,512]{1,0:T(8,128)(2,1)} %pad_maximum_fusion.1.refs_0_.refs_2_, bf16[4096,512]{1,0:T(8,128)(2,1)} %pad_maximum_fusion.2.refs_1_.refs_3_, ...), custom_call_target="tpu_custom_call" | custom-call | flops 4294967296 | bytes 12582912 | tf_op jit(solution)/shard_map/pallas_call | solution.py:93
  525.6 26.4 %shard_map.66 = bf16[1024,512]{1,0:T(8,128)(2,1)S(1)} custom-call(s32[6,4]{1,0:T(8,128)S(1)} %copy.54.bounds_ref, bf16[1024,1024]{1,0:T(8,128)(2,1)S(1)} %copy-done, bf16[4096,512]{1,0:T(8,128)(2,1)} %pad_maximum_fusion.1.refs_0_.refs_2_, bf16[4096,512]{1,0:T(8,128)(2,1)} %pad_maximum_fusion.2.refs_1_.refs_3_, ...), custom_call_target="tpu_custom_call" | custom-call | flops 4294967296 | bytes 12582912 | tf_op jit(solution)/shard_map/pallas_call | solution.py:93
  560.9 25.3 %shard_map.65 = bf16[1024,512]{1,0:T(8,128)(2,1)S(1)} custom-call(s32[6,4]{1,0:T(8,128)S(1)} %copy.49.bounds_ref, bf16[1024,1024]{1,0:T(8,128)(2,1)S(1)} %convolution_convert_fusion.q_ref, bf16[4096,512]{1,0:T(8,128)(2,1)} %pad_maximum_fusion.1.refs_0_.refs_2_, bf16[4096,512]{1,0:T(8,128)(2,1)} %pad_maximum_fusion.2.refs_1_.refs_3_, ...), custom_call_target="tpu_custom_call" | custom-call | flops 4294967296 | bytes 12582912 | tf_op jit(solution)/shard_map/pallas_call | solution.py:93
  587.1 4.8 collective-permute-done.13.refs_10_
  592.5 25.3 %shard_map.64 = bf16[1024,512]{1,0:T(8,128)(2,1)S(1)} custom-call(s32[6,4]{1,0:T(8,128)S(1)} %copy.49.bounds_ref, bf16[1024,1024]{1,0:T(8,128)(2,1)S(1)} %convolution_convert_fusion.q_ref, bf16[4096,512]{1,0:T(8,128)(2,1)} %pad_maximum_fusion.1.refs_0_.refs_2_, bf16[4096,512]{1,0:T(8,128)(2,1)} %pad_maximum_fusion.2.refs_1_.refs_3_, ...), custom_call_target="tpu_custom_call" | custom-call | flops 4294967296 | bytes 12582912 | tf_op jit(solution)/shard_map/pallas_call | solution.py:93
  617.9 16.8 %collective-permute-start.9 = (bf16[256,512]{1,0:T(8,128)(2,1)S(1)}, bf16[256,512]{1,0:T(8,128)(2,1)S(1)}, u32[]{:S(2)}, u32[]{:S(2)}) collective-permute-start(bf16[256,512]{1,0:T(8,128)(2,1)S(1)} %get-tuple-element.33), channel_id=1, source_target_pairs={{0,4},{4,0},{8,12},{12,8},{1,5},{5,1},{9,13},{13,9},{2,6},{6,2},{1... | collective-permute-start | bytes 786440 | tf_op jit(solution)/shard_map/ppermute | solution.py:164
  634.8 9.0 %collective-permute-done.9.refs_5_ = bf16[256,512]{1,0:T(8,128)(2,1)S(1)} collective-permute-done((bf16[256,512]{1,0:T(8,128)(2,1)S(1)}, bf16[256,512]{1,0:T(8,128)(2,1)S(1)}, u32[]{:S(2)}, u32[]{:S(2)}) %collective-permute-start.9) | collective-permute-done | bytes 262176 | tf_op jit(solution)/shard_map/ppermute | solution.py:164
  648.2 10.7 %collective-permute-done.7.refs_2_ = bf16[256,512]{1,0:T(8,128)(2,1)S(1)} collective-permute-done((bf16[256,512]{1,0:T(8,128)(2,1)S(1)}, bf16[256,512]{1,0:T(8,128)(2,1)S(1)}, u32[]{:S(2)}, u32[]{:S(2)}) %collective-permute-start.7) | collective-permute-done | bytes 262176 | tf_op jit(solution)/shard_map/ppermute | solution.py:164
  659.5 14.4 %shard_map.68.refs_26_ = bf16[512,4096]{1,0:T(8,128)(2,1)} custom-call(s32[2]{0:T(128)S(1)} %pad_add_fusion.rank_ref, bf16[256,512]{1,0:T(8,128)(2,1)S(1)} %get-tuple-element.38.refs_0_, bf16[256,512]{1,0:T(8,128)(2,1)S(1)} %collective-permute-done.6.refs_1_, bf16[256,512]{1,0:T(8,128)(2,1)S(1)} %collective-permute-done.7.refs_2_, ...), custom_call_target="tpu_custom_call" | custom-call | flops 8589934592 | bytes 25165824 | tf_op jit(solution)/shard_map/pallas_call | solution.py:148
  676.5 14.1 %shard_map.69 = bf16[512,4096]{1,0:T(8,128)(2,1)} custom-call(s32[2]{0:T(128)S(1)} %pad_add_fusion.rank_ref, bf16[256,512]{1,0:T(8,128)(2,1)S(1)} %get-tuple-element.38.refs_0_, bf16[256,512]{1,0:T(8,128)(2,1)S(1)} %collective-permute-done.6.refs_1_, bf16[256,512]{1,0:T(8,128)(2,1)S(1)} %collective-permute-done.7.refs_2_, ...), custom_call_target="tpu_custom_call", output_to_operand_aliasing={{}: (27, {})} | custom-call | flops 8589934592 | bytes 25165824 | tf_op jit(solution)/shard_map/pallas_call | solution.py:148
  (149 shorter events, 62.7 us)
Async XLA Ops:
  6.5 54.0 %all-gather.14.cloned.1.call-start = ((), (), s32[]{:S(2)}) async-start(), calls=%async_computation.3 | async-start | bytes 2621440 | tf_op jit(solution)/shard_map/all_gather | solution.py:184
  8.9 95.2 %all-gather.12.cloned.1.call-start = ((), (), s32[]{:S(2)}) async-start(), calls=%async_computation.2 | async-start | bytes 2621440 | tf_op jit(solution)/shard_map/all_gather | solution.py:184
  9.6 244.5 %all-gather.8.cloned.1.call-start = ((), (), s32[]{:S(2)}) async-start(), calls=%async_computation | async-start | bytes 10485760 | tf_op jit(solution)/shard_map/all_gather | solution.py:197
  14.3 389.0 %all-gather.10.cloned.1.call-start = ((), (), s32[]{:S(2)}) async-start(), calls=%async_computation.1 | async-start | bytes 10485760 | tf_op jit(solution)/shard_map/all_gather | solution.py:197
  60.6 61.7 %collective-permute-start.30 = (bf16[4,128,2048]{2,1,0:T(8,128)(2,1)}, bf16[4,128,2048]{2,1,0:T(8,128)(2,1)}, u32[]{:S(2)}, u32[]{:S(2)}) collective-permute-start(bf16[4,128,2048]{2,1,0:T(8,128)(2,1)} %bitcast.32.refs_16_), channel_id=1, source_target_pairs={{0,16},{16,0},{1,17},{17,1},{2,18},{18,2},{3,19},{19,3},{4,20},{20... | collective-permute-start | bytes 6291464 | tf_op jit(solution)/shard_map/ppermute | solution.py:164
  62.0 63.3 %collective-permute-start.28 = (bf16[4,128,2048]{2,1,0:T(8,128)(2,1)}, bf16[4,128,2048]{2,1,0:T(8,128)(2,1)}, u32[]{:S(2)}, u32[]{:S(2)}) collective-permute-start(bf16[4,128,2048]{2,1,0:T(8,128)(2,1)} %bitcast.32.refs_16_), channel_id=1, source_target_pairs={{0,2},{1,3},{2,0},{3,1},{4,6},{5,7},{6,4},{7,5},{8,10},{9,11},{10,... | collective-permute-start | bytes 6291464 | tf_op jit(solution)/shard_map/ppermute | solution.py:164
  104.1 47.5 %collective-permute-start.21 = (bf16[4,128,2048]{2,1,0:T(8,128)(2,1)}, bf16[4,128,2048]{2,1,0:T(8,128)(2,1)}, u32[]{:S(2)}, u32[]{:S(2)}) collective-permute-start(bf16[4,128,2048]{2,1,0:T(8,128)(2,1)} %bitcast.90), channel_id=1, source_target_pairs={{0,16},{16,0},{1,17},{17,1},{2,18},{18,2},{3,19},{19,3},{4,20},{20... | collective-permute-start | bytes 6291464 | tf_op jit(solution)/shard_map/ppermute | solution.py:164
  105.5 48.8 %collective-permute-start.19 = (bf16[4,128,2048]{2,1,0:T(8,128)(2,1)}, bf16[4,128,2048]{2,1,0:T(8,128)(2,1)}, u32[]{:S(2)}, u32[]{:S(2)}) collective-permute-start(bf16[4,128,2048]{2,1,0:T(8,128)(2,1)} %bitcast.91), channel_id=1, source_target_pairs={{0,2},{1,3},{2,0},{3,1},{4,6},{5,7},{6,4},{7,5},{8,10},{9,11},{10,... | collective-permute-start | bytes 6291464 | tf_op jit(solution)/shard_map/ppermute | solution.py:164
  122.3 311.0 %collective-permute-start.27 = (bf16[4,128,2048]{2,1,0:T(8,128)(2,1)}, bf16[4,128,2048]{2,1,0:T(8,128)(2,1)}, u32[]{:S(2)}, u32[]{:S(2)}) collective-permute-start(bf16[4,128,2048]{2,1,0:T(8,128)(2,1)} %bitcast.32.refs_16_), channel_id=1, source_target_pairs={{0,1},{1,0},{2,3},{3,2},{4,5},{5,4},{6,7},{7,6},{8,9},{9,8},{10,11... | collective-permute-start | bytes 6291464 | tf_op jit(solution)/shard_map/ppermute | solution.py:164
  124.6 347.5 %collective-permute-start.32 = (bf16[2,128,2048]{2,1,0:T(8,128)(2,1)}, bf16[2,128,2048]{2,1,0:T(8,128)(2,1)}, u32[]{:S(2)}, u32[]{:S(2)}) collective-permute-start(bf16[2,128,2048]{2,1,0:T(8,128)(2,1)} %slice.64), channel_id=1, source_target_pairs={{0,2},{1,3},{2,0},{3,1},{4,6},{5,7},{6,4},{7,5},{8,10},{9,11},{10,... | collective-permute-start | bytes 3145736 | tf_op jit(solution)/shard_map/ppermute | solution.py:164
  415.0 58.7 %collective-permute-start.3 = (bf16[1024,512]{1,0:T(8,128)(2,1)}, bf16[1024,512]{1,0:T(8,128)(2,1)}, u32[]{:S(2)}, u32[]{:S(2)}) collective-permute-start(bf16[1024,512]{1,0:T(8,128)(2,1)} %fusion), channel_id=1, source_target_pairs={{0,1},{1,0},{2,3},{3,2},{4,5},{5,4},{6,7},{7,6},{8,9},{9,8},{10,11... | collective-permute-start | bytes 3145736 | tf_op jit(solution)/shard_map/ppermute | solution.py:164
  420.5 40.9 %collective-permute-start.1 = (bf16[1024,512]{1,0:T(8,128)(2,1)}, bf16[1024,512]{1,0:T(8,128)(2,1)}, u32[]{:S(2)}, u32[]{:S(2)}) collective-permute-start(bf16[1024,512]{1,0:T(8,128)(2,1)} %convolution_convert_fusion.2), channel_id=1, source_target_pairs={{0,2},{1,3},{2,0},{3,1},{4,6},{5,7},{6,4},{7,5},{8,10},{9,11},{10,... | collective-permute-start | bytes 3145736 | tf_op jit(solution)/shard_map/ppermute | solution.py:164
  433.2 41.9 %collective-permute-start = (bf16[1024,512]{1,0:T(8,128)(2,1)}, bf16[1024,512]{1,0:T(8,128)(2,1)}, u32[]{:S(2)}, u32[]{:S(2)}) collective-permute-start(bf16[1024,512]{1,0:T(8,128)(2,1)} %convolution_convert_fusion.2), channel_id=1, source_target_pairs={{0,1},{1,0},{2,3},{3,2},{4,5},{5,4},{6,7},{7,6},{8,9},{9,8},{10,11... | collective-permute-start | bytes 3145736 | tf_op jit(solution)/shard_map/ppermute | solution.py:164
  439.9 35.3 %collective-permute-start.5 = (bf16[1024,512]{1,0:T(8,128)(2,1)}, bf16[1024,512]{1,0:T(8,128)(2,1)}, u32[]{:S(2)}, u32[]{:S(2)}) collective-permute-start(bf16[1024,512]{1,0:T(8,128)(2,1)} %collective-permute-done.4), channel_id=1, source_target_pairs={{0,1},{1,0},{2,3},{3,2},{4,5},{5,4},{6,7},{7,6},{8,9},{9,8},{10,11... | collective-permute-start | bytes 3145736 | tf_op jit(solution)/shard_map/ppermute | solution.py:164
  475.2 81.3 %collective-permute-start.29 = (bf16[4,128,2048]{2,1,0:T(8,128)(2,1)}, bf16[4,128,2048]{2,1,0:T(8,128)(2,1)S(1)}, u32[]{:S(2)}, u32[]{:S(2)}) collective-permute-start(bf16[4,128,2048]{2,1,0:T(8,128)(2,1)} %collective-permute-done.28.refs_18_), channel_id=1, source_target_pairs={{0,1},{1,0},{2,3},{3,2},{4,5},{5,4},{6,7},{7,6},{8,9},{9,8},{10,11... | collective-permute-start | bytes 6291464 | tf_op jit(solution)/shard_map/ppermute | solution.py:164
  475.2 81.3 %collective-permute-start.31 = (bf16[4,128,2048]{2,1,0:T(8,128)(2,1)}, bf16[4,128,2048]{2,1,0:T(8,128)(2,1)S(1)}, u32[]{:S(2)}, u32[]{:S(2)}) collective-permute-start(bf16[4,128,2048]{2,1,0:T(8,128)(2,1)} %collective-permute-done.30.refs_20_), channel_id=1, source_target_pairs={{0,1},{1,0},{2,3},{3,2},{4,5},{5,4},{6,7},{7,6},{8,9},{9,8},{10,11... | collective-permute-start | bytes 6291464 | tf_op jit(solution)/shard_map/ppermute | solution.py:164
  479.4 46.1 %collective-permute-start.24 = (bf16[2,128,2048]{2,1,0:T(8,128)(2,1)S(1)}, bf16[2,128,2048]{2,1,0:T(8,128)(2,1)S(1)}, u32[]{:S(2)}, u32[]{:S(2)}) collective-permute-start(bf16[2,128,2048]{2,1,0:T(8,128)(2,1)S(1)} %copy-done.3), channel_id=1, source_target_pairs={{0,16},{16,0},{1,17},{17,1},{2,18},{18,2},{3,19},{19,3},{4,20},{20... | collective-permute-start | bytes 3145736 | tf_op jit(solution)/shard_map/ppermute | solution.py:164
  498.5 53.6 %collective-permute-start.34 = (bf16[2,128,2048]{2,1,0:T(8,128)(2,1)}, bf16[2,128,2048]{2,1,0:T(8,128)(2,1)}, u32[]{:S(2)}, u32[]{:S(2)}) collective-permute-start(bf16[2,128,2048]{2,1,0:T(8,128)(2,1)} %collective-permute-done.32.refs_22_), channel_id=1, source_target_pairs={{0,1},{1,0},{2,3},{3,2},{4,5},{5,4},{6,7},{7,6},{8,9},{9,8},{10,11... | collective-permute-start | bytes 3145736 | tf_op jit(solution)/shard_map/ppermute | solution.py:164
  499.2 54.0 %collective-permute-start.35 = (bf16[2,128,2048]{2,1,0:T(8,128)(2,1)S(1)}, bf16[2,128,2048]{2,1,0:T(8,128)(2,1)}, u32[]{:S(2)}, u32[]{:S(2)}) collective-permute-start(bf16[2,128,2048]{2,1,0:T(8,128)(2,1)S(1)} %collective-permute-done.33.refs_23_), channel_id=1, source_target_pairs={{0,1},{1,0},{2,3},{3,2},{4,5},{5,4},{6,7},{7,6},{8,9},{9,8},{10,11... | collective-permute-start | bytes 3145736 | tf_op jit(solution)/shard_map/ppermute | solution.py:164
  556.5 35.3 %collective-permute-start.13 = (bf16[256,512]{1,0:T(8,128)(2,1)S(1)}, bf16[256,512]{1,0:T(8,128)(2,1)S(1)}, u32[]{:S(2)}, u32[]{:S(2)}) collective-permute-start(bf16[256,512]{1,0:T(8,128)(2,1)S(1)} %get-tuple-element.28), channel_id=1, source_target_pairs={{0,8},{4,12},{8,0},{12,4},{1,9},{5,13},{9,1},{13,5},{2,10},{6,14},... | collective-permute-start | bytes 786440 | tf_op jit(solution)/shard_map/ppermute | solution.py:164
  586.4 87.5 %collective-permute-start.18 = (bf16[4,128,2048]{2,1,0:T(8,128)(2,1)S(1)}, bf16[4,128,2048]{2,1,0:T(8,128)(2,1)S(1)}, u32[]{:S(2)}, u32[]{:S(2)}) collective-permute-start(bf16[4,128,2048]{2,1,0:T(8,128)(2,1)S(1)} %bitcast.93), channel_id=1, source_target_pairs={{0,1},{1,0},{2,3},{3,2},{4,5},{5,4},{6,7},{7,6},{8,9},{9,8},{10,11... | collective-permute-start | bytes 6291464 | tf_op jit(solution)/shard_map/ppermute | solution.py:164
  586.5 87.4 %collective-permute-start.20 = (bf16[4,128,2048]{2,1,0:T(8,128)(2,1)}, bf16[4,128,2048]{2,1,0:T(8,128)(2,1)S(1)}, u32[]{:S(2)}, u32[]{:S(2)}) collective-permute-start(bf16[4,128,2048]{2,1,0:T(8,128)(2,1)} %collective-permute-done.19.refs_18_), channel_id=1, source_target_pairs={{0,1},{1,0},{2,3},{3,2},{4,5},{5,4},{6,7},{7,6},{8,9},{9,8},{10,11... | collective-permute-start | bytes 6291464 | tf_op jit(solution)/shard_map/ppermute | solution.py:164
  587.0 87.0 %collective-permute-start.22 = (bf16[4,128,2048]{2,1,0:T(8,128)(2,1)}, bf16[4,128,2048]{2,1,0:T(8,128)(2,1)}, u32[]{:S(2)}, u32[]{:S(2)}) collective-permute-start(bf16[4,128,2048]{2,1,0:T(8,128)(2,1)} %collective-permute-done.21.refs_20_), channel_id=1, source_target_pairs={{0,1},{1,0},{2,3},{3,2},{4,5},{5,4},{6,7},{7,6},{8,9},{9,8},{10,11... | collective-permute-start | bytes 6291464 | tf_op jit(solution)/shard_map/ppermute | solution.py:164
  591.8 42.9 %collective-permute-start.11 = (bf16[256,512]{1,0:T(8,128)(2,1)S(1)}, bf16[256,512]{1,0:T(8,128)(2,1)S(1)}, u32[]{:S(2)}, u32[]{:S(2)}) collective-permute-start(bf16[256,512]{1,0:T(8,128)(2,1)S(1)} %get-tuple-element.31), channel_id=1, source_target_pairs={{0,12},{4,8},{8,4},{12,0},{1,13},{5,9},{9,5},{13,1},{2,14},{6,10},... | collective-permute-start | bytes 786440 | tf_op jit(solution)/shard_map/ppermute | solution.py:164
  (35 other events, 766.2 us)
Sparse Core Ops, SparseCore 0:
  9.0 48.9 all-gather.13
  59.5 44.4 all-gather.11
  105.6 148.4 all-gather.7
  255.5 147.7 all-gather.9

commit v2 on v1

v2 whole, which is shorter than its diff:
```python
import functools
import math

import jax
import jax.numpy as jnp
from jax import lax
from jax.experimental import pallas as pl
from jax.experimental.pallas import tpu as pltpu
from jax.sharding import PartitionSpec as P


NEG_BIG = -1e30
SUBS = 2


def flash_kernel(n_cp, n_tp, group, n_parts, first_bit, exp_scale, bounds_ref, *refs):
    q_refs, k_refs, v_refs = refs[:n_parts], refs[n_parts:2 * n_parts], refs[2 * n_parts:3 * n_parts]
    start_ref = refs[3 * n_parts]
    o_refs = refs[3 * n_parts + 1:-4]
    q_all, m_ref, l_ref, acc_ref = refs[-4:]
    step_idx = pl.program_id(0)
    dest, sub = step_idx // SUBS, step_idx % SUBS
    tile = jnp.bitwise_xor(bounds_ref[6, 0], first_bit - dest) * SUBS + sub
    head_dim = q_all.shape[1]
    rows = start_ref.shape[0]
    per_piece = n_tp // 2
    for sub_idx in range(SUBS):
        @pl.when(sub == sub_idx)
        def _():
            begin = 0
            for ref in q_refs:
                first = max(begin, sub_idx * rows)
                last = min(begin + ref.shape[0], (sub_idx + 1) * rows)
                if first < last:
                    for head in range(group):
                        at = head * rows + first - sub_idx * rows
                        q_all[at:at + last - first, :] = ref[first - begin:last - begin, head * head_dim:(head + 1) * head_dim]
                begin += ref.shape[0]
    m_ref[...] = jnp.full_like(m_ref, NEG_BIG)
    l_ref[...] = jnp.zeros_like(l_ref)
    acc_ref[...] = jnp.zeros_like(acc_ref)
    first_pos = bounds_ref[0, tile]
    lo = bounds_ref[1, tile]
    mid = bounds_ref[2, tile]
    full_end = bounds_ref[3, tile]
    hi = bounds_ref[4, tile]
    cp_rank = bounds_ref[5, 0]

    def block(masked, blk):
        piece = blk // per_piece
        early = piece < n_cp
        owner = jnp.where(early, piece, 2 * n_cp - 1 - piece)
        slot = jnp.bitwise_xor(owner, cp_rank)
        chunk = slot * n_tp + blk % per_piece + jnp.where(early, 0, per_piece)

        def rows_of(part_refs):
            sizes = [ref.shape[0] // (n_cp * n_tp) for ref in part_refs]
            return jnp.concatenate([ref[pl.ds(pl.multiple_of(chunk * size, size), size), :] for ref, size in zip(part_refs, sizes)], axis=0)

        k_blk = rows_of(k_refs)
        v_blk = rows_of(v_refs)
        width = k_blk.shape[0]
        scores = lax.dot_general(q_all[...], k_blk, (((1,), (1,)), ((), ())), preferred_element_type=jnp.float32) * exp_scale
        if masked:
            key_pos = blk * width + lax.broadcasted_iota(jnp.int32, (rows, width), 1)
            row_pos = first_pos + lax.broadcasted_iota(jnp.int32, (rows, width), 0)
            allowed = (key_pos >= start_ref[...]) & (key_pos <= row_pos)
            scores = jnp.where(allowed[None], scores.reshape(group, rows, width), NEG_BIG).reshape(group * rows, width)
        m_old = m_ref[...]
        m_new = jnp.maximum(m_old, jnp.max(scores, axis=1, keepdims=True))
        probs = [jnp.exp2(scores[:, j:j + head_dim] - m_new) for j in range(0, width, head_dim)]
        rescale = jnp.exp2(m_old - m_new)
        l_ref[...] = rescale * l_ref[...] + functools.reduce(jnp.add, probs)
        prob_blk = jnp.concatenate([prob.astype(jnp.bfloat16) for prob in probs], axis=1)
        acc_ref[...] = rescale * acc_ref[...] + jnp.dot(prob_blk, v_blk, preferred_element_type=jnp.float32)
        m_ref[...] = m_new

    def step(blk, carry):
        full = (blk >= mid) & (blk < full_end)
        pl.when(full)(functools.partial(block, False, blk))
        pl.when(jnp.logical_not(full))(functools.partial(block, True, blk))
        return carry

    lax.fori_loop(lo, hi, step, 0)
    out = (acc_ref[...] / jnp.sum(l_ref[...], axis=1, keepdims=True)).astype(jnp.bfloat16)
    for idx, o_ref in enumerate(o_refs):
        @pl.when(dest == idx)
        def _():
            at = pl.multiple_of(sub * rows, rows)
            for head in range(group):
                o_ref[pl.ds(at, rows), head * head_dim:(head + 1) * head_dim] = out[head * rows:(head + 1) * rows]


def flash(n_cp, n_tp, first_bit, q_parts, kv_parts, head_dim, bounds, row_start):
    sizes = [q_part.shape[0] // n_tp for q_part in q_parts]
    tile = sum(sizes)
    cols = q_parts[0].shape[1]
    group = cols // head_dim
    exp_scale = head_dim ** -0.5 * math.log2(math.e)
    rows = tile // SUBS
    stacked = group * rows
    n_keys = [part.shape[0] for part in kv_parts]
    n_parts = len(sizes)
    grid_spec = pltpu.PrefetchScalarGridSpec(
        num_scalar_prefetch=1,
        grid=(2 * SUBS,),
        in_specs=[pl.BlockSpec((size, cols), lambda i, b: (jnp.bitwise_xor(b[6, 0], first_bit - i // SUBS), 0)) for size in sizes]
        + [pl.BlockSpec((keys, head_dim), lambda i, b: (0, 0)) for keys in n_keys]
        + [pl.BlockSpec((keys, head_dim), lambda i, b: (0, 1)) for keys in n_keys]
        + [pl.BlockSpec((rows, 1), lambda i, b: (jnp.bitwise_xor(b[6, 0], first_bit - i // SUBS) * SUBS + i % SUBS, 0))],
        out_specs=[pl.BlockSpec((tile, cols), lambda i, b: (0, 0))] * 2,
        scratch_shapes=[
            pltpu.VMEM((stacked, head_dim), jnp.bfloat16),
            pltpu.VMEM((stacked, head_dim), jnp.float32),
            pltpu.VMEM((stacked, head_dim), jnp.float32),
            pltpu.VMEM((stacked, head_dim), jnp.float32),
        ],
    )
    n_scores = stacked * SUBS * sum(n_keys)
    return pl.pallas_call(
        functools.partial(flash_kernel, n_cp, n_tp, group, n_parts, first_bit, exp_scale),
        grid_spec=grid_spec,
        out_shape=[jax.ShapeDtypeStruct((tile, cols), jnp.bfloat16)] * 2,
        compiler_params=pltpu.CompilerParams(dimension_semantics=("arbitrary",), vmem_limit_bytes=56 << 20),
        cost_estimate=pl.CostEstimate(flops=4 * n_scores * head_dim, bytes_accessed=12 << 20, transcendentals=n_scores),
    )(bounds, *q_parts, *kv_parts, *kv_parts, row_start)


def project_kernel(n_tp, heads, n_o, n_w, n_left, rank_ref, *refs):
    o_refs, sides = refs[:n_o], (refs[n_o:n_o + n_w], refs[n_o + n_w:n_o + 2 * n_w])
    y_ref, o_full = refs[-2:]
    n_cols = y_ref.shape[-1]
    head_dim = sides[0][0].shape[1]
    n_mates = n_o // n_tp

    @pl.when(pl.program_id(0) == 0)
    def _():
        for mate in range(n_mates):
            kv_idx = jnp.bitwise_xor(rank_ref[2], mate)
            for bit in range(n_tp):
                piece = o_refs[mate * n_tp + bit]
                source = jnp.bitwise_xor(rank_ref[0], bit)
                for head in range(heads):
                    part = jnp.bitwise_xor(rank_ref[1], kv_idx * heads + head)
                    col = pl.multiple_of((part * n_tp + source) * head_dim, head_dim)
                    o_full[:, pl.ds(col, head_dim)] = piece[:, head * head_dim:(head + 1) * head_dim]

    def columns(w_refs):
        total = None
        start = 0
        for w_ref in w_refs:
            depth = w_ref.shape[0] * head_dim
            term = jnp.dot(o_full[:, start:start + depth], w_ref[...].reshape(depth, n_cols), preferred_element_type=jnp.float32)
            total = term if total is None else total + term
            start += depth
        y_ref[...] = total.astype(y_ref.dtype)

    left = pl.program_id(0) < n_left
    pl.when(left)(functools.partial(columns, sides[0]))
    pl.when(jnp.logical_not(left))(functools.partial(columns, sides[1]))


def project(ranks, n_tp, pieces, w_sides, heads, n_cols=256):
    head_dim = w_sides[0][0].shape[1]
    rows, piece_cols = pieces[0].shape
    depth = sum(part.shape[0] for part in w_sides[0]) * head_dim
    n_left, n_right = [side[0].shape[2] // n_cols for side in w_sides]
    d_model = (n_left + n_right) * n_cols
    grid_spec = pltpu.PrefetchScalarGridSpec(
        num_scalar_prefetch=1,
        grid=(n_left + n_right,),
        in_specs=[pl.BlockSpec((rows, piece_cols), lambda i, t: (0, 0))] * len(pieces)
        + [pl.BlockSpec((part.shape[0], head_dim, n_cols), lambda i, t: (0, 0, jnp.minimum(i, n_left - 1))) for part in w_sides[0]]
        + [pl.BlockSpec((part.shape[0], head_dim, n_cols), lambda i, t: (0, 0, jnp.maximum(i - n_left, 0))) for part in w_sides[1]],
        out_specs=pl.BlockSpec((rows, n_cols), lambda i, t: (0, i)),
        scratch_shapes=[pltpu.VMEM((rows, depth), jnp.bfloat16)],
    )
    return pl.pallas_call(
        functools.partial(project_kernel, n_tp, heads, len(pieces), len(w_sides[0]), n_left),
        grid_spec=grid_spec,
        out_shape=jax.ShapeDtypeStruct((rows, d_model), jnp.bfloat16),
        compiler_params=pltpu.CompilerParams(dimension_semantics=("arbitrary",), vmem_limit_bytes=48 << 20),
        cost_estimate=pl.CostEstimate(flops=2 * rows * depth * d_model, bytes_accessed=40 << 20, transcendentals=0),
        name="project",
    )(ranks, *pieces, *w_sides[0], *w_sides[1])


def solution(mesh):
    n_cp = mesh.shape["cp"]
    n_tp = mesh.shape["tp"]
    n_dp = mesh.shape["dp"]

    def swap(arr, axis, bit):
        return lax.ppermute(arr, axis, [(src, src ^ bit) for src in range(mesh.shape[axis])])

    def send_rows(arr, mate, bit):
        perm = [(tp * n_cp + cp, (tp ^ bit) * n_cp + (cp ^ mate)) for tp in range(n_tp) for cp in range(n_cp)]
        return lax.ppermute(arr, ("tp", "cp"), perm) if mate or bit else arr

    calls = [(first_bit, mate) for first_bit in range(n_tp - 1, 0, -2) for mate in (1, 0)]

    def per_device(x_loc, seg_loc, w_q, w_k, w_v, w_o):
        cp_rank = lax.axis_index("cp")
        tp_rank = lax.axis_index("tp")
        own_rows, d_model = x_loc.shape
        kv_loc = w_k.shape[1]
        head_dim = w_k.shape[2]
        n_rows = own_rows * n_tp
        piece_len = n_rows // 2
        width = w_q.shape[1] * head_dim
        cuts = [0, own_rows * 3 // 4, own_rows]

        part_rows = w_o.shape[0] * head_dim // (n_dp * n_cp)
        part_idx = lax.axis_index("dp") * n_cp + cp_rank
        w_o_part = lax.dynamic_slice_in_dim(w_o.reshape(width, d_model), part_idx * part_rows, part_rows)
        col_cuts = [0, d_model // 4, d_model]
        mid_tp = n_tp // 2

        def gather_wo(side):
            w_tp = lax.all_gather(w_o_part[:, col_cuts[side]:col_cuts[side + 1]], "tp", axis=0)
            w_dp = swap(w_tp, "dp", 1)
            w_cp = swap(w_tp, "cp", 2)
            w_diag0 = swap(w_dp[:mid_tp], "cp", 2)
            w_diag1 = swap(w_cp[mid_tp:], "dp", 1)
            near = [w_tp, w_cp, w_dp, w_diag0, w_diag1]
            far = []
            for part in near:
                far.append(swap(part, "cp", 1))
            return [near[0], far[0], near[1], far[1], near[2], far[2], near[3], near[4], far[3], far[4]]

        x_parts = []
        for first, last in zip(cuts, cuts[1:]):
            x_parts.append(lax.all_gather(x_loc[first:last], "tp", axis=0, tiled=True))
        w_sides = [gather_wo(side) for side in range(2)]
        seg_all = lax.all_gather(seg_loc, ("cp", "tp"), axis=0, tiled=True)
        core = cp_rank % 2
        heads_per_kv = w_q.shape[1] // kv_loc
        w_q_heads = w_q.reshape(d_model, kv_loc, heads_per_kv * head_dim)
        w_q_keep, w_q_send = [lax.dynamic_index_in_dim(w_q_heads, core ^ mate, 1, False) for mate in range(2)]
        w_kv_keep, w_kv_send = [jnp.concatenate([lax.dynamic_index_in_dim(arr, core ^ mate, 1, False) for arr in (w_k, w_v)], axis=1) for mate in range(2)]

        tile_rows = own_rows // SUBS
        tile_row = jnp.arange(n_tp * SUBS) * tile_rows
        bounds, row_starts = [], []
        for mate in range(2):
            block = cp_rank ^ mate
            seg_rows = lax.dynamic_slice_in_dim(seg_all, block * n_rows, n_rows)
            row_start = jnp.sum((seg_all[None, :] < seg_rows[:, None]).astype(jnp.int32), axis=1)
            first_pos = jnp.where(tile_row < piece_len, block * piece_len + tile_row, (2 * n_cp - 1 - block) * piece_len + tile_row - piece_len)
            start_tiles = row_start.reshape(n_tp * SUBS, tile_rows)
            lo = start_tiles[:, 0] // own_rows
            full_end = first_pos // own_rows
            mid = jnp.minimum((start_tiles[:, -1] + own_rows - 1) // own_rows, full_end)
            bounds.append(jnp.stack([first_pos, lo, mid, full_end, full_end + 1, jnp.full_like(lo, cp_rank), jnp.full_like(lo, tp_rank)]).astype(jnp.int32))
            row_starts.append(row_start.reshape(-1, 1))
        x_parts[0], w_q_keep, w_q_send, w_kv_keep, w_kv_send, bounds, row_starts = lax.optimization_barrier((x_parts[0], w_q_keep, w_q_send, w_kv_keep, w_kv_send, bounds, row_starts))

        def rows_by(x_part, weights):
            return jnp.dot(x_part, weights, preferred_element_type=jnp.float32).astype(jnp.bfloat16)

        q_parts, kv_parts = [], []
        for x_part in x_parts:
            kv_send = rows_by(x_part, w_kv_send)
            kv_mate = swap(kv_send, "cp", 1)
            kv_keep = rows_by(x_part, w_kv_keep)
            kv_near = jnp.concatenate([kv_keep, kv_mate], axis=0)
            kv_far = swap(kv_near, "cp", 2)
            q_send = rows_by(x_part, w_q_send)
            q_mate = swap(q_send, "cp", 1)
            q_keep = rows_by(x_part, w_q_keep)
            q_parts.append((q_keep, q_mate))
            kv_parts.append(jnp.concatenate([kv_near, kv_far], axis=0))

        pieces = [None] * (2 * n_tp)
        for first_bit, mate in calls:
            tiles = flash(n_cp, n_tp, first_bit, [pair[mate] for pair in q_parts], kv_parts, head_dim, bounds[mate], row_starts[mate])
            for bit, mine in zip((first_bit, first_bit - 1), tiles):
                pieces[mate * n_tp + bit] = send_rows(mine, mate, bit)
        ranks = jnp.stack([tp_rank, part_idx, core]).astype(jnp.int32)
        return project(ranks, n_tp, pieces, w_sides, heads_per_kv)


    return jax.shard_map(
        per_device,
        mesh=mesh,
        in_specs=(P(("dp", "cp", "tp"), None), P(("dp", "cp", "tp")), P(None, "tp", None), P(None, "tp", None), P(None, "tp", None), P("tp", None, None)),
        out_specs=P(("dp", "cp", "tp"), None),
        check_vma=False,
    )
```

time: 707 us -> 746 us (1.055)
  the two profiles are of different devices: /device:TPU:0 before, /device:TPU:15 now
where the time goes in v2:
time: 746 us; the launch traced here: 736 us
  waiting for transfers between devices  350 us (47%)
  Pallas kernels  140 us (19%)
  local copies, waits for them, and re-layouts  75.6 us (10%)
  matrix products  55 us (7%)
  starting transfers between devices  45.1 us (6%)
  blocking collectives  29.8 us (4%)
  other arithmetic  27.4 us (4%)
  between operations  13.8 us (2%)
    all_gather x2, waiting for transfers between devices, per_device(): x_parts.append(lax.all_gather(x_loc[first:last], 'tp', axis=0, tiled=True))  176 us
    pallas_call x4, Pallas kernels, flash(): pl.pallas_call(functools.partial(flash_kernel, n_cp, n_tp, group, n_parts...  112 us
    ppermute x24, waiting for transfers between devices, swap(): lax.ppermute(arr, axis, [(src, src ^ bit) for src in range(mesh.shape[axi...  109 us
    dot_general x8, matrix products, rows_by(): jnp.dot(x_part, weights, preferred_element_type=jnp.float32)  55 us
    ppermute x7, waiting for transfers between devices, send_rows(): return lax.ppermute(arr, ('tp', 'cp'), perm) if mate or bit else arr  52.1 us
    ppermute x7, starting transfers between devices, send_rows(): return lax.ppermute(arr, ('tp', 'cp'), perm) if mate or bit else arr  33 us
    all_gather x1, blocking collectives, per_device(): seg_all = lax.all_gather(seg_loc, ('cp', 'tp'), axis=0, tiled=True)  29.8 us
    pallas_call x1, Pallas kernels, project(): pl.pallas_call(functools.partial(project_kernel, n_tp, heads, len(pieces)...  27.6 us
  transfers between devices with their start and end apart: 35, of which 12 were waited for; matrix products, arithmetic and copies ran while one was open for 21% of the time, Pallas kernels for 15%

profile of v2, /device:TPU:15, one launch (start us, length us, event | category | flops | bytes accessed | tf_op | source)
XLA Modules:
  0.0 736.5 jit_solution(656719041274147450)
XLA Ops:
  16.8 29.8 %all-gather.2 = s32[16,1,512]{2,1,0:T(1,128)S(1)} all-gather(s32[1,1,512]{2,1,0:T(1,128)S(1)} %bitcast.100), channel_id=1, replica_groups=mesh['dp'=2,'tp'=4,'cp'=4] {'cp','tp'}, dimensions={0}, use_global_device_ids=true | all-gather | bytes 34816 | tf_op jit(solution)/shard_map/all_gather | solution.py:235
  46.6 15.8 %convert_reduce_fusion = (s32[2048]{0:T(1024)S(1)}, s32[2048]{0:T(1024)S(1)}) fusion(s32[8192]{0:T(1024)S(1)} %bitcast.97, s32[2048]{0:T(1024)S(1)} %get-tuple-element.58, s32[2048]{0:T(1024)S(1)} %get-tuple-element.57), kind=kLoop, calls=%fused_computation | loop fusion | flops 100659200 | bytes 65536 | tf_op jit(solution)/shard_map/reduce_sum | solution.py:248
  62.4 9.1 %all-gather.14.cloned.1.call-done = bf16[512,3072]{1,0:T(8,128)(2,1)} async-done(((bf16[128,3072]{1,0:T(8,128)(2,1)}), bf16[512,3072]{1,0:T(8,128)(2,1)}) %all-gather.14.cloned.1.call-update) | async-done | bytes 3145744 | tf_op jit(solution)/shard_map/all_gather | solution.py:220
  72.1 11.6 %constant_dynamic-slice_fusion.1 = (bf16[4096,1,128]{2,1,0:T(2,128)(2,1)}, bf16[4096,1,128]{2,1,0:T(2,128)(2,1)S(1)}, bf16[4096,1,128]{2,1,0:T(2,128)(2,1)S(1)}, bf16[4096,1,128]{2,1,0:T(2,128)(2,1)S(1)}) fusion(bf16[4096,2,128]{2,1,0:T(2,128)(2,1)} %param.10, s32[]{:T(128)S(6)} %select_n.152, s32[]{:T(128)S(6)} %select_n.151, bf16[4096,2,128]{2,1,0:T(2,128)(2,1)} %param.9), kind=kLoop, calls=%fused_computation.37 | loop fusion | bytes 8388616 | tf_op jit(solution)/shard_map/jit(dynamic_index_in_dim)/dynamic_slice | solution.py:240
  84.9 11.9 %copy.53 = bf16[4096,8,128]{0,2,1:T(8,128)(2,1)} copy(bf16[4096,8,128]{2,1,0:T(8,128)(2,1)} %param.8) | data formatting | bytes 16777216 | tf_op args[2]
  104.7 8.6 %constant_dynamic-slice_fusion.5 = (bf16[4096,1,512]{0,2,1:T(8,128)(2,1)}, bf16[4096,1,512]{0,2,1:T(8,128)(2,1)}) fusion(bf16[4096,2,512]{0,2,1:T(8,128)(2,1)} %bitcast.85, s32[]{:T(128)S(6)} %select_n.152, s32[]{:T(128)S(6)} %select_n.151), kind=kLoop, calls=%fused_computation.41 | loop fusion | bytes 16777224 | tf_op jit(solution)/shard_map/jit(dynamic_index_in_dim)/dynamic_slice | solution.py:239
  113.3 49.7 %collective-permute-done.16.refs_12_ = bf16[4,128,1024]{2,1,0:T(8,128)(2,1)} collective-permute-done((bf16[4,128,1024]{2,1,0:T(8,128)(2,1)}, bf16[4,128,1024]{2,1,0:T(8,128)(2,1)}, u32[]{:S(2)}, u32[]{:S(2)}) %collective-permute-start.16) | collective-permute-done | bytes 1048608 | tf_op jit(solution)/shard_map/ppermute | solution.py:194
  193.7 124.7 %all-gather.8.cloned.1.call-done = bf16[1536,4096]{1,0:T(8,128)(2,1)} async-done(((bf16[384,4096]{1,0:T(8,128)(2,1)}), bf16[1536,4096]{1,0:T(8,128)(2,1)}) %all-gather.8.cloned.1.call-update) | async-done | bytes 12582928 | tf_op jit(solution)/shard_map/all_gather | solution.py:233
  318.4 9.7 %convolution_convert_fusion.2 = bf16[1536,256]{1,0:T(8,128)(2,1)} fusion(bf16[1536,4096]{1,0:T(8,128)(2,1)} %all-gather.8.cloned.1.call-done, bf16[4096,256]{1,0:T(8,128)(2,1)} %pad_maximum_fusion.2), kind=kOutput, calls=%fused_computation.5 | convolution fusion | flops 3221618688 | bytes 15466496 | tf_op jit(solution)/shard_map/dot_general | solution.py:259
  328.8 19.0 %convolution_convert_fusion = bf16[1536,512]{1,0:T(8,128)(2,1)} fusion(bf16[1536,4096]{1,0:T(8,128)(2,1)S(1)} %copy-done.11, bf16[4096,512]{1,0:T(8,128)(2,1)S(1)} %bitcast.88), kind=kOutput, calls=%fused_computation.3 | convolution fusion | flops 6443237376 | bytes 18350080 | tf_op jit(solution)/shard_map/dot_general | solution.py:259
  347.8 51.2 %all-gather.10.cloned.1.call-done = bf16[512,4096]{1,0:T(8,128)(2,1)} async-done(((bf16[128,4096]{1,0:T(8,128)(2,1)}), bf16[512,4096]{1,0:T(8,128)(2,1)}) %all-gather.10.cloned.1.call-update) | async-done | bytes 4194320 | tf_op jit(solution)/shard_map/all_gather | solution.py:233
  404.4 10.9 %convolution_convert_fusion.1.refs_0_ = bf16[1536,512]{1,0:T(8,128)(2,1)} fusion(bf16[1536,4096]{1,0:T(8,128)(2,1)} %all-gather.8.cloned.1.call-done, bf16[4096,512]{1,0:T(8,128)(2,1)S(1)} %bitcast.86), kind=kOutput, calls=%fused_computation.4 | convolution fusion | flops 6443237376 | bytes 18350080 | tf_op jit(solution)/shard_map/dot_general | solution.py:259
  443.2 24.7 %collective-permute-done.1 = bf16[3072,256]{1,0:T(8,128)(2,1)} collective-permute-done((bf16[3072,256]{1,0:T(8,128)(2,1)}, bf16[3072,256]{1,0:T(8,128)(2,1)}, u32[]{:S(2)}, u32[]{:S(2)}) %collective-permute-start.1) | collective-permute-done | bytes 1572896 | tf_op jit(solution)/shard_map/ppermute | solution.py:194
  473.6 28.1 %collective-permute-done.27.refs_24_ = bf16[2,128,3072]{2,1,0:T(8,128)(2,1)} collective-permute-done((bf16[2,128,3072]{2,1,0:T(8,128)(2,1)}, bf16[2,128,3072]{2,1,0:T(8,128)(2,1)}, u32[]{:S(2)}, u32[]{:S(2)}) %collective-permute-start.27) | collective-permute-done | bytes 1572896 | tf_op jit(solution)/shard_map/ppermute | solution.py:194
  502.8 34.4 %shard_map.65 = (bf16[512,512]{1,0:T(8,128)(2,1)}, bf16[512,512]{1,0:T(8,128)(2,1)}) custom-call(s32[7,8]{1,0:T(8,128)} %stack.32.bounds_ref, bf16[1536,512]{1,0:T(8,128)(2,1)} %convolution_convert_fusion.1.refs_0_, bf16[512,512]{1,0:T(8,128)(2,1)} %fusion.refs_1_, bf16[6144,256]{1,0:T(8,128)(2,1)} %pad_maximum_fusion.refs_2_.refs_4_, ...), custom_call_target="tpu_custom_call" | custom-call | flops 8589934592 | bytes 12582912 | tf_op jit(solution)/shard_map/pallas_call | solution.py:120
  537.2 34.7 %shard_map.64 = (bf16[512,512]{1,0:T(8,128)(2,1)}, bf16[512,512]{1,0:T(8,128)(2,1)}) custom-call(s32[7,8]{1,0:T(8,128)} %stack.32.bounds_ref, bf16[1536,512]{1,0:T(8,128)(2,1)} %convolution_convert_fusion.1.refs_0_, bf16[512,512]{1,0:T(8,128)(2,1)} %fusion.refs_1_, bf16[6144,256]{1,0:T(8,128)(2,1)} %pad_maximum_fusion.refs_2_.refs_4_, ...), custom_call_target="tpu_custom_call" | custom-call | flops 8589934592 | bytes 12582912 | tf_op jit(solution)/shard_map/pallas_call | solution.py:120
  571.9 16.1 %shard_map.67 = (bf16[512,512]{1,0:T(8,128)(2,1)}, bf16[512,512]{1,0:T(8,128)(2,1)}) custom-call(s32[7,8]{1,0:T(8,128)} %stack.33.bounds_ref, bf16[1536,512]{1,0:T(8,128)(2,1)} %collective-permute-done.7.refs_0_, bf16[512,512]{1,0:T(8,128)(2,1)} %collective-permute-done.8.refs_1_, bf16[6144,256]{1,0:T(8,128)(2,1)} %pad_maximum_fusion.refs_2_.refs_4_, ...), custom_call_target="tpu_custom_call" | custom-call | flops 8589934592 | bytes 12582912 | tf_op jit(solution)/shard_map/pallas_call | solution.py:120
  589.8 20.6 %collective-permute-start.11 = (bf16[512,512]{1,0:T(8,128)(2,1)}, bf16[512,512]{1,0:T(8,128)(2,1)S(1)}, u32[]{:S(2)}, u32[]{:S(2)}) collective-permute-start(bf16[512,512]{1,0:T(8,128)(2,1)} %get-tuple-element.37), channel_id=1, source_target_pairs={{0,9},{1,8},{2,11},{3,10},{4,13},{5,12},{6,15},{7,14},{8,1},{9,0},... | collective-permute-start | bytes 1572872 | tf_op jit(solution)/shard_map/ppermute | solution.py:198
  610.7 27.1 %shard_map.66 = (bf16[512,512]{1,0:T(8,128)(2,1)}, bf16[512,512]{1,0:T(8,128)(2,1)}) custom-call(s32[7,8]{1,0:T(8,128)} %stack.33.bounds_ref, bf16[1536,512]{1,0:T(8,128)(2,1)} %collective-permute-done.7.refs_0_, bf16[512,512]{1,0:T(8,128)(2,1)} %collective-permute-done.8.refs_1_, bf16[6144,256]{1,0:T(8,128)(2,1)} %pad_maximum_fusion.refs_2_.refs_4_, ...), custom_call_target="tpu_custom_call" | custom-call | flops 8589934592 | bytes 12582912 | tf_op jit(solution)/shard_map/pallas_call | solution.py:120
  637.8 9.0 %collective-permute-start.10 = (bf16[512,512]{1,0:T(8,128)(2,1)}, bf16[512,512]{1,0:T(8,128)(2,1)S(1)}, u32[]{:S(2)}, u32[]{:S(2)}) collective-permute-start(bf16[512,512]{1,0:T(8,128)(2,1)} %get-tuple-element.36), channel_id=1, source_target_pairs={{0,5},{1,4},{2,7},{3,6},{4,1},{5,0},{6,3},{7,2},{8,13},{9,12},{10,... | collective-permute-start | bytes 1572872 | tf_op jit(solution)/shard_map/ppermute | solution.py:198
  649.9 7.1 collective-permute-done.12.refs_7_
  661.7 28.3 %collective-permute-done.5.refs_2_ = bf16[512,512]{1,0:T(8,128)(2,1)S(1)} collective-permute-done((bf16[512,512]{1,0:T(8,128)(2,1)}, bf16[512,512]{1,0:T(8,128)(2,1)S(1)}, u32[]{:S(2)}, u32[]{:S(2)}) %collective-permute-start.5) | collective-permute-done | bytes 524320 | tf_op jit(solution)/shard_map/ppermute | solution.py:198
  689.9 12.1 %collective-permute-done.6.refs_3_ = bf16[512,512]{1,0:T(8,128)(2,1)S(1)} collective-permute-done((bf16[512,512]{1,0:T(8,128)(2,1)}, bf16[512,512]{1,0:T(8,128)(2,1)S(1)}, u32[]{:S(2)}, u32[]{:S(2)}) %collective-permute-start.6) | collective-permute-done | bytes 524320 | tf_op jit(solution)/shard_map/ppermute | solution.py:198
  702.0 27.6 %project.1 = bf16[512,4096]{1,0:T(8,128)(2,1)} custom-call(s32[3]{0:T(128)S(1)} %pad_add_fusion.rank_ref, bf16[512,512]{1,0:T(8,128)(2,1)S(1)} %copy-done, bf16[512,512]{1,0:T(8,128)(2,1)S(1)} %collective-permute-done.4.refs_1_, bf16[512,512]{1,0:T(8,128)(2,1)S(1)} %collective-permute-done.5.refs_2_, bf16[512,512]{1,0:T(8,128)(2,1)S(1)} %collective-permute-done.6.refs_3_, ...), custom_call_target="tpu_custom_call" | custom-call | flops 17179869184 | bytes 41943040 | tf_op jit(solution)/shard_map/project/pallas_call | solution.py:178
  (145 shorter events, 101.0 us)
Async XLA Ops:
  6.5 64.9 %all-gather.14.cloned.1.call-start = ((), (), s32[]{:S(2)}) async-start(), calls=%async_computation.3 | async-start | bytes 3932160 | tf_op jit(solution)/shard_map/all_gather | solution.py:220
  8.6 92.7 %all-gather.12.cloned.1.call-start = ((), (), s32[]{:S(2)}) async-start(), calls=%async_computation.2 | async-start | bytes 1310720 | tf_op jit(solution)/shard_map/all_gather | solution.py:220
  10.4 308.0 %all-gather.8.cloned.1.call-start = ((), (), s32[]{:S(2)}) async-start(), calls=%async_computation | async-start | bytes 15728640 | tf_op jit(solution)/shard_map/all_gather | solution.py:233
  14.4 384.7 %all-gather.10.cloned.1.call-start = ((), (), s32[]{:S(2)}) async-start(), calls=%async_computation.1 | async-start | bytes 5242880 | tf_op jit(solution)/shard_map/all_gather | solution.py:233
  71.5 116.9 %collective-permute-start.25 = (bf16[4,128,3072]{2,1,0:T(8,128)(2,1)}, bf16[4,128,3072]{2,1,0:T(8,128)(2,1)}, u32[]{:S(2)}, u32[]{:S(2)}) collective-permute-start(bf16[4,128,3072]{2,1,0:T(8,128)(2,1)} %bitcast.103), channel_id=1, source_target_pairs={{0,16},{16,0},{1,17},{17,1},{2,18},{18,2},{3,19},{19,3},{4,20},{20... | collective-permute-start | bytes 9437192 | tf_op jit(solution)/shard_map/ppermute | solution.py:194
  71.7 119.3 %collective-permute-start.23 = (bf16[4,128,3072]{2,1,0:T(8,128)(2,1)}, bf16[4,128,3072]{2,1,0:T(8,128)(2,1)}, u32[]{:S(2)}, u32[]{:S(2)}) collective-permute-start(bf16[4,128,3072]{2,1,0:T(8,128)(2,1)} %bitcast.104), channel_id=1, source_target_pairs={{0,2},{1,3},{2,0},{3,1},{4,6},{5,7},{6,4},{7,5},{8,10},{9,11},{10,... | collective-permute-start | bytes 9437192 | tf_op jit(solution)/shard_map/ppermute | solution.py:194
  101.3 61.7 %collective-permute-start.16 = (bf16[4,128,1024]{2,1,0:T(8,128)(2,1)}, bf16[4,128,1024]{2,1,0:T(8,128)(2,1)}, u32[]{:S(2)}, u32[]{:S(2)}) collective-permute-start(bf16[4,128,1024]{2,1,0:T(8,128)(2,1)} %bitcast.19.refs_8_), channel_id=1, source_target_pairs={{0,16},{16,0},{1,17},{17,1},{2,18},{18,2},{3,19},{19,3},{4,20},{20... | collective-permute-start | bytes 3145736 | tf_op jit(solution)/shard_map/ppermute | solution.py:194
  101.6 63.6 %collective-permute-start.14 = (bf16[4,128,1024]{2,1,0:T(8,128)(2,1)}, bf16[4,128,1024]{2,1,0:T(8,128)(2,1)}, u32[]{:S(2)}, u32[]{:S(2)}) collective-permute-start(bf16[4,128,1024]{2,1,0:T(8,128)(2,1)} %bitcast.19.refs_8_), channel_id=1, source_target_pairs={{0,2},{1,3},{2,0},{3,1},{4,6},{5,7},{6,4},{7,5},{8,10},{9,11},{10,... | collective-permute-start | bytes 3145736 | tf_op jit(solution)/shard_map/ppermute | solution.py:194
  185.5 241.2 %collective-permute-start.13 = (bf16[4,128,1024]{2,1,0:T(8,128)(2,1)}, bf16[4,128,1024]{2,1,0:T(8,128)(2,1)}, u32[]{:S(2)}, u32[]{:S(2)}) collective-permute-start(bf16[4,128,1024]{2,1,0:T(8,128)(2,1)} %bitcast.19.refs_8_), channel_id=1, source_target_pairs={{0,1},{1,0},{2,3},{3,2},{4,5},{5,4},{6,7},{7,6},{8,9},{9,8},{10,11... | collective-permute-start | bytes 3145736 | tf_op jit(solution)/shard_map/ppermute | solution.py:194
  187.8 239.8 %collective-permute-start.20 = (bf16[2,128,1024]{2,1,0:T(8,128)(2,1)S(1)}, bf16[2,128,1024]{2,1,0:T(8,128)(2,1)S(1)}, u32[]{:S(2)}, u32[]{:S(2)}) collective-permute-start(bf16[2,128,1024]{2,1,0:T(8,128)(2,1)S(1)} %collective-permute-done.18.refs_14_), channel_id=1, source_target_pairs={{0,1},{1,0},{2,3},{3,2},{4,5},{5,4},{6,7},{7,6},{8,9},{9,8},{10,11... | collective-permute-start | bytes 1572872 | tf_op jit(solution)/shard_map/ppermute | solution.py:194
  187.9 239.8 %collective-permute-start.21 = (bf16[2,128,1024]{2,1,0:T(8,128)(2,1)S(1)}, bf16[2,128,1024]{2,1,0:T(8,128)(2,1)}, u32[]{:S(2)}, u32[]{:S(2)}) collective-permute-start(bf16[2,128,1024]{2,1,0:T(8,128)(2,1)S(1)} %collective-permute-done.19.refs_15_), channel_id=1, source_target_pairs={{0,1},{1,0},{2,3},{3,2},{4,5},{5,4},{6,7},{7,6},{8,9},{9,8},{10,11... | collective-permute-start | bytes 1572872 | tf_op jit(solution)/shard_map/ppermute | solution.py:194
  422.4 45.5 %collective-permute-start.1 = (bf16[3072,256]{1,0:T(8,128)(2,1)}, bf16[3072,256]{1,0:T(8,128)(2,1)}, u32[]{:S(2)}, u32[]{:S(2)}) collective-permute-start(bf16[3072,256]{1,0:T(8,128)(2,1)} %pad_maximum_fusion.3), channel_id=1, source_target_pairs={{0,2},{1,3},{2,0},{3,1},{4,6},{5,7},{6,4},{7,5},{8,10},{9,11},{10,... | collective-permute-start | bytes 4718600 | tf_op jit(solution)/shard_map/ppermute | solution.py:194
  426.8 46.3 %collective-permute-start.15 = (bf16[4,128,1024]{2,1,0:T(8,128)(2,1)}, bf16[4,128,1024]{2,1,0:T(8,128)(2,1)}, u32[]{:S(2)}, u32[]{:S(2)}) collective-permute-start(bf16[4,128,1024]{2,1,0:T(8,128)(2,1)} %collective-permute-done.14.refs_10_), channel_id=1, source_target_pairs={{0,1},{1,0},{2,3},{3,2},{4,5},{5,4},{6,7},{7,6},{8,9},{9,8},{10,11... | collective-permute-start | bytes 3145736 | tf_op jit(solution)/shard_map/ppermute | solution.py:194
  427.7 74.0 %collective-permute-start.27 = (bf16[2,128,3072]{2,1,0:T(8,128)(2,1)}, bf16[2,128,3072]{2,1,0:T(8,128)(2,1)}, u32[]{:S(2)}, u32[]{:S(2)}) collective-permute-start(bf16[2,128,3072]{2,1,0:T(8,128)(2,1)} %slice.54), channel_id=1, source_target_pairs={{0,2},{1,3},{2,0},{3,1},{4,6},{5,7},{6,4},{7,5},{8,10},{9,11},{10,... | collective-permute-start | bytes 4718600 | tf_op jit(solution)/shard_map/ppermute | solution.py:194
  434.9 67.8 %collective-permute-start.28 = (bf16[2,128,3072]{2,1,0:T(8,128)(2,1)}, bf16[2,128,3072]{2,1,0:T(8,128)(2,1)}, u32[]{:S(2)}, u32[]{:S(2)}) collective-permute-start(bf16[2,128,3072]{2,1,0:T(8,128)(2,1)} %slice.55), channel_id=1, source_target_pairs={{0,16},{16,0},{1,17},{17,1},{2,18},{18,2},{3,19},{19,3},{4,20},{20... | collective-permute-start | bytes 4718600 | tf_op jit(solution)/shard_map/ppermute | solution.py:194
  467.9 120.1 %collective-permute-start.22 = (bf16[4,128,3072]{2,1,0:T(8,128)(2,1)}, bf16[4,128,3072]{2,1,0:T(8,128)(2,1)S(1)}, u32[]{:S(2)}, u32[]{:S(2)}) collective-permute-start(bf16[4,128,3072]{2,1,0:T(8,128)(2,1)} %bitcast.105), channel_id=1, source_target_pairs={{0,1},{1,0},{2,3},{3,2},{4,5},{5,4},{6,7},{7,6},{8,9},{9,8},{10,11... | collective-permute-start | bytes 9437192 | tf_op jit(solution)/shard_map/ppermute | solution.py:194
  473.1 173.7 %collective-permute-start.24 = (bf16[4,128,3072]{2,1,0:T(8,128)(2,1)}, bf16[4,128,3072]{2,1,0:T(8,128)(2,1)}, u32[]{:S(2)}, u32[]{:S(2)}) collective-permute-start(bf16[4,128,3072]{2,1,0:T(8,128)(2,1)} %collective-permute-done.23.refs_20_), channel_id=1, source_target_pairs={{0,1},{1,0},{2,3},{3,2},{4,5},{5,4},{6,7},{7,6},{8,9},{9,8},{10,11... | collective-permute-start | bytes 9437192 | tf_op jit(solution)/shard_map/ppermute | solution.py:194
  473.1 174.3 %collective-permute-start.26 = (bf16[4,128,3072]{2,1,0:T(8,128)(2,1)}, bf16[4,128,3072]{2,1,0:T(8,128)(2,1)}, u32[]{:S(2)}, u32[]{:S(2)}) collective-permute-start(bf16[4,128,3072]{2,1,0:T(8,128)(2,1)} %collective-permute-done.25.refs_22_), channel_id=1, source_target_pairs={{0,1},{1,0},{2,3},{3,2},{4,5},{5,4},{6,7},{7,6},{8,9},{9,8},{10,11... | collective-permute-start | bytes 9437192 | tf_op jit(solution)/shard_map/ppermute | solution.py:194
  501.6 70.3 %collective-permute-start.7 = (bf16[1536,512]{1,0:T(8,128)(2,1)S(1)}, bf16[1536,512]{1,0:T(8,128)(2,1)}, u32[]{:S(2)}, u32[]{:S(2)}) collective-permute-start(bf16[1536,512]{1,0:T(8,128)(2,1)S(1)} %copy-done.14), channel_id=1, source_target_pairs={{0,1},{1,0},{2,3},{3,2},{4,5},{5,4},{6,7},{7,6},{8,9},{9,8},{10,11... | collective-permute-start | bytes 4718600 | tf_op jit(solution)/shard_map/ppermute | solution.py:194
  537.2 73.2 %collective-permute-start.29 = (bf16[2,128,3072]{2,1,0:T(8,128)(2,1)}, bf16[2,128,3072]{2,1,0:T(8,128)(2,1)S(1)}, u32[]{:S(2)}, u32[]{:S(2)}) collective-permute-start(bf16[2,128,3072]{2,1,0:T(8,128)(2,1)} %collective-permute-done.27.refs_24_), channel_id=1, source_target_pairs={{0,1},{1,0},{2,3},{3,2},{4,5},{5,4},{6,7},{7,6},{8,9},{9,8},{10,11... | collective-permute-start | bytes 4718600 | tf_op jit(solution)/shard_map/ppermute | solution.py:194
  571.9 65.9 %collective-permute-start.30 = (bf16[2,128,3072]{2,1,0:T(8,128)(2,1)}, bf16[2,128,3072]{2,1,0:T(8,128)(2,1)S(1)}, u32[]{:S(2)}, u32[]{:S(2)}) collective-permute-start(bf16[2,128,3072]{2,1,0:T(8,128)(2,1)} %collective-permute-done.28.refs_25_), channel_id=1, source_target_pairs={{0,1},{1,0},{2,3},{3,2},{4,5},{5,4},{6,7},{7,6},{8,9},{9,8},{10,11... | collective-permute-start | bytes 4718600 | tf_op jit(solution)/shard_map/ppermute | solution.py:194
  589.8 59.1 %collective-permute-start.11 = (bf16[512,512]{1,0:T(8,128)(2,1)}, bf16[512,512]{1,0:T(8,128)(2,1)S(1)}, u32[]{:S(2)}, u32[]{:S(2)}) collective-permute-start(bf16[512,512]{1,0:T(8,128)(2,1)} %get-tuple-element.37), channel_id=1, source_target_pairs={{0,9},{1,8},{2,11},{3,10},{4,13},{5,12},{6,15},{7,14},{8,1},{9,0},... | collective-permute-start | bytes 1572872 | tf_op jit(solution)/shard_map/ppermute | solution.py:198
  610.4 46.6 %collective-permute-start.12 = (bf16[512,512]{1,0:T(8,128)(2,1)}, bf16[512,512]{1,0:T(8,128)(2,1)S(1)}, u32[]{:S(2)}, u32[]{:S(2)}) collective-permute-start(bf16[512,512]{1,0:T(8,128)(2,1)} %get-tuple-element.38), channel_id=1, source_target_pairs={{0,13},{1,12},{2,15},{3,14},{4,9},{5,8},{6,11},{7,10},{8,5},{9,4},... | collective-permute-start | bytes 1572872 | tf_op jit(solution)/shard_map/ppermute | solution.py:198
  648.9 53.1 %collective-permute-start.6 = (bf16[512,512]{1,0:T(8,128)(2,1)}, bf16[512,512]{1,0:T(8,128)(2,1)S(1)}, u32[]{:S(2)}, u32[]{:S(2)}) collective-permute-start(bf16[512,512]{1,0:T(8,128)(2,1)} %get-tuple-element.31), channel_id=1, source_target_pairs={{0,12},{1,13},{2,14},{3,15},{4,8},{5,9},{6,10},{7,11},{8,4},{9,5},... | collective-permute-start | bytes 1572872 | tf_op jit(solution)/shard_map/ppermute | solution.py:198
  (31 other events, 646.8 us)
Sparse Core Ops, SparseCore 0:
  8.9 62.5 all-gather.13
  73.0 28.2 all-gather.11
  102.9 215.4 all-gather.7
  319.8 79.2 all-gather.9
